TPU v7x, 32 devices: a whole 2x2x4 slice. The times are simulated.
32 devices in a mesh: section: 4 (over y, x), vocab: 8 (over z, core).
Axes of the slice: x: 2, y: 2, z: 4, core: 2. Of those that a mesh axis runs over, the one named last changes fastest.
Arguments:
- hidden: bfloat16 [512, 4608], P('section', 'vocab'), may hold values from -6 to 6
- slab: bfloat16 [16384, 4608], P('vocab', 'section'), may hold values from -0.29882812 to 0.29882812
- token_ids: int32 [512], P('section'), may hold values from 0 to 16383
- target_ids: int32 [512], P('section'), may hold values from 0 to 16383
- input_cot: bfloat16 [512, 4608], P('section', 'vocab'), may hold values from -0.3984375 to 0.3984375
- loss_grad: float32 [512], P('section'), may hold values from 2 to 32
Outputs:
- token_loss: float32 [512], P('section')
- hidden_grad: bfloat16 [512, 4608], P('section', 'vocab')
- tied_grad: bfloat16 [16384, 4608], P('vocab', 'section')
All inputs are finite; a program needn't handle non-finite values.
Results may differ from a plain program's by a relative error of at most 0.0047.
Values may be sent and summed in bfloat16 or wider, within the bound.
A program may use at most 64 MiB of HBM per device.

v0:
```python
import functools
import math

import jax
import jax.numpy as jnp
from jax import lax
from jax.experimental import pallas as pl
from jax.experimental.pallas import tpu as pltpu
from jax.sharding import PartitionSpec as P

logit_cap = 30.0
code_knee = 16.0
code_top = 32767.0
f32 = jnp.float32
bf16 = jnp.bfloat16


def encode(x):
    y = x / (jnp.abs(x) + code_knee) * code_top
    return jnp.floor(y + 0.5).astype(jnp.int32).astype(jnp.int16)


def decode(code):
    y = code.astype(jnp.int32).astype(f32) * (1.0 / code_top)
    return code_knee * y / (1.0 - jnp.abs(y))


def over_tokens(left, right):
    return lax.dot_general(
        left, right, (((1,), (1,)), ((), ())), preferred_element_type=jnp.float32
    )


def fused_kernel(
    dims, hid_hbm, cot_hbm, slab_hbm, tok_hbm, tgt_hbm, scale_hbm, loss, hgrad, tied,
    hid, cot, tok, tgt, scale,
    slab, zg, hq, hm, h, snd, rcv, own, cq, cm, cf, ids, tid_tx, cap, ex, stat_tx, stat_rx,
    dl, gt, px_rx, gs, zr, fin,
    in_sem, zr_s, zr_r, zl_s, zl_r, pl_s, pl_r, mt_s, mt_r, cp_s, cp_r, cr_s, cl_s, cz_r,
    cm_s, cm_r, id_s, id_r, rs_s, rs_r, st_s, st_r, ag_s, ag_r, px_s, px_r, g_s, g_r, f_s, f_r,
):
    S, V = dims
    Z = V // 2
    W, T = hid.shape
    R, Q = slab.shape
    half = R // 2
    s = lax.axis_index("section")
    v = lax.axis_index("vocab")
    z = v // 2
    c = v % 2
    mate = z * 2 + 1 - c
    nx, ny, far = s ^ 1, s ^ 2, s ^ 3
    tile = 256

    def rc(src, dst, ssem, rsem, dev):
        return pltpu.make_async_remote_copy(
            src_ref=src, dst_ref=dst, send_sem=ssem, recv_sem=rsem,
            device_id=dev, device_id_type=pl.DeviceIdType.MESH,
        )

    def got(ref, rsem):
        rc(ref, ref, rsem, rsem, (s, mate)).wait_recv()

    def sent(ref, ssem):
        rc(ref, ref, ssem, ssem, (s, mate)).wait_send()

    loads = [
        pltpu.make_async_copy(src, dst, in_sem.at[i])
        for i, (src, dst) in enumerate(
            ((hid_hbm, hid), (cot_hbm, cot), (tok_hbm, tok), (tgt_hbm, tgt), (scale_hbm, scale), (slab_hbm, slab))
        )
    ]
    for load in loads:
        load.start()

    bar = pltpu.get_barrier_semaphore()
    for r in range(1, S):
        pl.semaphore_signal(bar, inc=1, device_id=((s + r) % S, v), device_id_type=pl.DeviceIdType.MESH)
    for r in range(1, V):
        pl.semaphore_signal(bar, inc=1, device_id=(s, (v + r) % V), device_id_type=pl.DeviceIdType.MESH)
    for load in loads[:5]:
        load.wait()
    tid_tx[...] = jnp.broadcast_to(tok[...], tid_tx.shape)
    ids[s] = jnp.broadcast_to(tok[...], tid_tx.shape)
    pl.semaphore_wait(bar, S + V - 2)

    def z_send(k):
        b = z - k

        @pl.when((z < Z - 1) & (b >= 0))
        def _():
            rc(hid if k == 0 else zg.at[b], zg.at[b], zr_s.at[k], zr_r.at[k], (s, v + 2)).start()

        d = z + k

        @pl.when((z > 0) & (d <= Z - 1))
        def _():
            rc(hid if k == 0 else zg.at[d], zg.at[d], zl_s.at[k], zl_r.at[k], (s, v - 2)).start()

    def plane_send(b, src):
        @pl.when(b != s)
        def _():
            rc(src, hq.at[s], pl_s.at[b], pl_r.at[s], (b, v)).start()

        @pl.when(b == s)
        def _():
            rc(src, hm.at[s], mt_s.at[s], mt_r.at[s], (s, mate)).start()
            hq[s] = src[...]

    z_send(0)
    plane_send(z, hid)

    @pl.when(s != z)
    def _():
        rc(cot, cq.at[s], cp_s, cp_r.at[s], (z, v)).start()

    for r in range(1, S):
        t = (s + r) % S
        rc(tid_tx, ids.at[s], id_s.at[r - 1], id_r.at[s], (t, v)).start()

    for k in range(Z - 1):
        b = z - 1 - k
        d = z + 1 + k

        @pl.when(b >= 0)
        def _():
            got(zg.at[b], zr_r.at[k])

        @pl.when(d <= Z - 1)
        def _():
            got(zg.at[d], zl_r.at[k])

        if k + 1 < Z - 1:
            z_send(k + 1)

        @pl.when(b >= 0)
        def _():
            plane_send(b, zg.at[b])

        @pl.when(d <= Z - 1)
        def _():
            plane_send(d, zg.at[d])

    for r in range(1, S):
        t = (s + r) % S
        got(hq.at[t], pl_r.at[t])
        rc(hq.at[t], hm.at[t], mt_s.at[t], mt_r.at[t], (s, mate)).start()

    def assemble(full, mine, other, t):
        cols = slice(t % 2 * T, (t % 2 + 1) * T)
        full[t // 2, pl.ds(pl.multiple_of(c * W, 16), W), cols] = mine[t]
        full[t // 2, pl.ds(pl.multiple_of((1 - c) * W, 16), W), cols] = other[t]

    for t in range(S):
        got(hm.at[t], mt_r.at[t])
        assemble(h, hq, hm, t)
    loads[5].wait()

    def forward(src, t):
        @pl.when((z >= s) & (z < Z - 1))
        def _():
            rc(src, cq.at[t], cr_s.at[t], cz_r.at[t], (s, v + 2)).start()

        @pl.when((z <= s) & (z > 0))
        def _():
            rc(src, cq.at[t], cl_s.at[t], cz_r.at[t], (s, v - 2)).start()

        rc(src, cm.at[t], cm_s.at[t], cm_r.at[t], (s, mate)).start()

    @pl.when(z == s)
    def _():
        cq[s] = cot[...]
        forward(cot, s)
        for r in range(1, S):
            t = (s + r) % S
            got(cq.at[t], cp_r.at[t])
            forward(cq.at[t], t)

    low, high = slice(0, half), slice(half, R)

    def logits(p, last):
        def logit_tile(j, carry):
            rows = pl.ds(pl.multiple_of(j * tile, tile), tile)
            part = jnp.dot(slab[rows, :], h[p], preferred_element_type=f32)
            for m in range(2):
                snd[2 * p + m, rows, :] = encode(part[:, m * T:(m + 1) * T])
            if last:
                own[rows, :] = jnp.where(s % 2 == 0, part[:, :T], part[:, T:])
            return carry

        lax.fori_loop(0, R // tile, logit_tile, 0)

    def logit_send(n, t, slot, part, to):
        rc(snd.at[t, part], rcv.at[slot, part], rs_s.at[n], rs_r.at[n], (to, v)).start()

    def logit_got(n, slot, part):
        got(rcv.at[slot, part], rs_r.at[n])

    def relay(t, part):
        def relay_tile(j, carry):
            rows = pl.ds(pl.multiple_of(part.start + j * tile, tile), tile)
            snd[t, rows, :] = encode(decode(snd[t, rows, :]) + decode(rcv[2, rows, :]))
            return carry

        lax.fori_loop(0, half // tile, relay_tile, 0)

    other = 1 - s // 2
    logits(other, False)
    logit_send(0, far, 2, low, nx)
    logit_send(1, far, 2, high, ny)
    logit_send(2, ny, 1, high, ny)
    logits(s // 2, True)
    logit_send(3, nx, 0, low, nx)
    logit_got(0, 2, low)
    relay(ny, low)
    logit_send(4, ny, 1, low, ny)
    logit_got(1, 2, high)
    relay(nx, high)
    logit_send(5, nx, 0, high, nx)

    @pl.when(z != s)
    def _():
        for r in range(S):
            t = (s + r) % S
            got(cq.at[t], cz_r.at[t])
            forward(cq.at[t], t)

    for t in range(S):
        got(cm.at[t], cm_r.at[t])
        assemble(cf, cq, cm, t)

    logit_got(2, 1, high)
    logit_got(3, 0, low)
    logit_got(4, 1, low)
    logit_got(5, 0, high)
    soft = 128
    target = tgt[...]

    def row_ids(j, n, width):
        return v * R + j * n + lax.broadcasted_iota(jnp.int32, (n, width), 0)

    def soft_tile(j, carry):
        total, pick = carry
        rows = pl.ds(pl.multiple_of(j * soft, soft), soft)
        raw = own[rows, :] + decode(rcv[0, rows, :]) + decode(rcv[1, rows, :])
        capped = logit_cap * jnp.tanh(raw / logit_cap)
        e = jnp.exp(capped)
        cap[rows, :] = capped
        ex[rows, :] = e
        hit = row_ids(j, soft, T) == target
        total = total + jnp.sum(e, axis=0, keepdims=True)
        pick = pick + jnp.sum(jnp.where(hit, capped, 0.0), axis=0, keepdims=True)
        return total, pick

    zero = jnp.zeros((1, T), f32)
    total, pick = lax.fori_loop(0, R // soft, soft_tile, (zero, zero))
    stat_tx[0:8, :] = jnp.broadcast_to(total, (8, T))
    stat_tx[8:16, :] = jnp.broadcast_to(pick, (8, T))
    for r in range(1, V):
        rc(stat_tx, stat_rx.at[v], st_s.at[r - 1], st_r.at[v], (s, (v + r) % V)).start()
    stat_rx[v] = stat_tx[...]
    for r in range(1, V):
        u = (v + r) % V
        got(stat_rx.at[u], st_r.at[u])
    sums = stat_rx[0]
    for u in range(1, V):
        sums = sums + stat_rx[u]
    total = sums[0:1, :]
    loss[...] = jnp.log(total) - sums[8:9, :]
    gain = scale[...]

    def grad_tile(j, carry):
        rows = pl.ds(pl.multiple_of(j * soft, soft), soft)
        capped = cap[rows, :]
        hit = (row_ids(j, soft, T) == target).astype(f32)
        slope = 1.0 - (capped / logit_cap) ** 2
        dl[s, rows, :] = (gain * (ex[rows, :] / total - hit) * slope).astype(bf16)
        return carry

    lax.fori_loop(0, R // soft, grad_tile, 0)

    def grad_send(n, t, part, to):
        block = dl.at[t, part]
        rc(block, block, ag_s.at[n], ag_r.at[n], (to, v)).start()

    def grad_got(n, t, part):
        got(dl.at[t, part], ag_r.at[n])

    grad_send(0, s, high, nx)
    grad_send(1, s, low, ny)
    grad_send(2, s, low, nx)
    grad_send(3, s, high, ny)

    def term(t):
        g = lax.dot_general(
            dl[t], slab[...], (((0,), (0,)), ((), ())), preferred_element_type=f32
        )

        gt[t] = g.T
        give = gt.at[t, pl.ds(pl.multiple_of((1 - c) * W, 16), W)]
        rc(give, px_rx.at[t], px_s.at[t], px_r.at[t], (s, mate)).start()

    def fin_send(q, src):
        @pl.when(q != z)
        def _():
            rc(src, fin.at[z], f_s.at[q], f_r.at[z], (s, 2 * q + c)).start()

        @pl.when(q == z)
        def _():
            fin[z] = src[...]

    def pass_on(t, local):
        got(px_rx.at[t], px_r.at[t])
        kept = gt[t, pl.ds(pl.multiple_of(c * W, 16), W), :]
        gs[t] = (kept + px_rx[t]).astype(bf16)
        if local:
            fin_send(s, gs.at[t])
        else:
            rc(gs.at[t], zr.at[s], g_s.at[t], g_r.at[s], (t, v)).start()

    term(s)
    grad_got(1, ny, low)
    grad_send(4, ny, low, nx)
    grad_got(0, nx, high)
    grad_send(5, nx, high, ny)
    pass_on(s, True)
    grad_got(2, nx, low)
    term(nx)
    grad_got(3, ny, high)
    term(ny)
    pass_on(nx, False)
    pass_on(ny, False)
    grad_got(4, far, low)
    grad_got(5, far, high)
    term(far)
    pass_on(far, False)
    for r in range(1, S):
        q = s ^ r
        got(zr.at[q], g_r.at[q])
        fin_send(q, zr.at[q])

    for r in range(1, S):
        t = (s + r) % S
        got(ids.at[t], id_r.at[t])
    every = jnp.concatenate([ids[t][0:1, :] for t in range(S)], axis=1)
    root = math.sqrt(Q * S)

    def tied_tile(j, carry):
        rows = pl.ds(pl.multiple_of(j * tile, tile), tile)
        onehot = (row_ids(j, tile, S * T) == every).astype(f32).astype(bf16)
        head, embed = 0.0, 0.0
        for p in range(S // 2):
            lhs = jnp.concatenate([dl[2 * p, rows, :], dl[2 * p + 1, rows, :]], axis=1)
            head = head + over_tokens(lhs, h[p])
            embed = embed + over_tokens(onehot[:, 2 * p * T:2 * (p + 1) * T], cf[p])
        tied[rows, :] = (head + embed * root).astype(bf16)
        return carry

    lax.fori_loop(0, R // tile, tied_tile, 0)

    for r in range(1, Z):
        u = (z + r) % Z
        got(fin.at[u], f_r.at[u])
    acc = fin[0].astype(f32)
    for u in range(1, Z):
        acc = acc + fin[u].astype(f32)
    hgrad[...] = acc.astype(bf16)

    for k in range(Z - 1):
        @pl.when((z < Z - 1) & (z - k >= 0))
        def _():
            sent(hid, zr_s.at[k])

        @pl.when((z > 0) & (z + k <= Z - 1))
        def _():
            sent(hid, zl_s.at[k])
    for b in range(S):
        @pl.when(b != s)
        def _():
            sent(hid, pl_s.at[b])
            sent(gs.at[b], g_s.at[b])
        sent(hid, mt_s.at[b])
        sent(cot, cm_s.at[b])
        sent(px_rx.at[b], px_s.at[b])

        @pl.when((z >= s) & (z < Z - 1))
        def _():
            sent(cot, cr_s.at[b])

        @pl.when((z <= s) & (z > 0))
        def _():
            sent(cot, cl_s.at[b])
    for q in range(Z):
        @pl.when(q != z)
        def _():
            sent(gs.at[0], f_s.at[q])

    @pl.when(s != z)
    def _():
        sent(cot, cp_s)
    for r in range(1, S):
        sent(tid_tx, id_s.at[r - 1])
    for n in range(6):
        sent(snd.at[0, low], rs_s.at[n])
        sent(dl.at[0, low], ag_s.at[n])
    for r in range(1, V):
        sent(stat_tx, st_s.at[r - 1])


def put_out(loss, hgrad, tied, loss_out, hgrad_out, tied_out, sems):
    moves = [
        pltpu.make_async_copy(src, dst, sems.at[i])
        for i, (src, dst) in enumerate(((tied, tied_out), (hgrad, hgrad_out), (loss, loss_out)))
    ]
    for move in moves:
        move.start()
    for move in moves:
        move.wait()


def fused(hidden, slab, token_ids, target_ids, input_cot, loss_grad):
    S = lax.axis_size("section")
    V = lax.axis_size("vocab")
    Z = V // 2
    T, W = hidden.shape
    R, Q = slab.shape
    vm = pltpu.VMEM
    dma = pltpu.SemaphoreType.DMA
    half = vm((S, W, T), bf16)
    both = vm((S // 2, Q, 2 * T), bf16)
    scratch = [
        vm((W, T), bf16), vm((W, T), bf16),
        vm((1, T), jnp.int32), vm((1, T), jnp.int32), vm((1, T), f32),
        vm((R, Q), bf16), half, half, half, both,
        vm((S, R, T), jnp.int16), vm((3, R, T), jnp.int16), vm((R, T), f32),
        half, half, both, vm((S, 8, T), jnp.int32), vm((8, T), jnp.int32),
        vm((R, T), f32), vm((R, T), f32), vm((16, T), f32), vm((V, 16, T), f32),
        vm((S, R, T), bf16), vm((S, Q, T), f32), vm((S, W, T), f32), half, half, vm((Z, W, T), bf16),
        dma((6,)), dma((Z,)), dma((Z,)), dma((Z,)), dma((Z,)),
        dma((S,)), dma((S,)), dma((S,)), dma((S,)), dma, dma((S,)),
        dma((S,)), dma((S,)), dma((S,)), dma((S,)), dma((S,)), dma((S,)), dma((S,)),
        dma((6,)), dma((6,)), dma((V,)), dma((V,)), dma((6,)), dma((6,)),
        dma((S,)), dma((S,)), dma((S,)), dma((S,)), dma((Z,)), dma((Z,)),
    ]
    block = pl.BlockSpec(memory_space=vm)
    anywhere = pl.BlockSpec(memory_space=pl.ANY)
    results = pl.pallas_call(
        functools.partial(fused_kernel, (S, V)),
        out_shape=(
            jax.ShapeDtypeStruct((1, T), f32),
            jax.ShapeDtypeStruct((W, T), bf16),
            jax.ShapeDtypeStruct((R, Q), bf16),
        ),
        in_specs=[anywhere] * 6,
        out_specs=(block, block, block),
        scratch_shapes=scratch,
        compiler_params=pltpu.CompilerParams(
            collective_id=0, has_side_effects=True, vmem_limit_bytes=48 * 2**20
        ),
        name="fused",
    )(
        hidden.T, input_cot.T, slab,
        token_ids.reshape(1, T), target_ids.reshape(1, T), loss_grad.reshape(1, T),
    )
    loss, hgrad, tied = pl.pallas_call(
        put_out,
        out_shape=tuple(jax.ShapeDtypeStruct(x.shape, x.dtype) for x in results),
        in_specs=[block] * 3,
        out_specs=(anywhere,) * 3,
        scratch_shapes=[dma((3,))],
        compiler_params=pltpu.CompilerParams(vmem_limit_bytes=8 * 2**20),
        name="put_out",
    )(*results)
    return loss.reshape(T), hgrad.T, tied


def from_partner(block, axis, stride):
    count = lax.axis_size(axis)
    route = []
    for low in range(count):
        high = low | 1 << stride
        if high != low and high < count:
            route += [(low, high), (high, low)]
    return lax.ppermute(block, axis, route)


def left_product(left_side, right_side):
    return lax.dot_general(
        left_side, right_side, (((0,), (0,)), ((), ())), preferred_element_type=jnp.float32
    )


def local_parts(raw_logits, targets, columns):
    capped = logit_cap * jnp.tanh(raw_logits / logit_cap)
    exp_logits = jnp.exp(capped)
    target_hit = (targets[:, None] == columns[None, :]).astype(jnp.float32)
    local_total = jnp.sum(exp_logits, axis=1)
    local_pick = jnp.sum(target_hit * capped, axis=1)
    return (capped, exp_logits, target_hit, local_total, local_pick)


def finish(capped, exp_logits, target_hit, exp_total, picked, scales):
    token_loss = jnp.log(exp_total) - picked
    slope = 1.0 - (capped / logit_cap) ** 2
    dlogit = (scales[:, None] * (exp_logits / exp_total[:, None] - target_hit) * slope).astype(
        jnp.bfloat16
    )
    return (token_loss, dlogit)


def general(hidden, slab, token_ids, target_ids, input_cot, loss_grad):
    rows_here = slab.shape[0]
    quarter_width = slab.shape[1]
    sections = lax.axis_size("section")
    shards = lax.axis_size("vocab")
    model_width = quarter_width * sections
    own_tokens = hidden.shape[0]
    share_width = hidden.shape[1]
    full_hidden, full_cot = (
        lax.all_gather(hidden, "vocab", axis=1, tiled=True),
        lax.all_gather(input_cot, "vocab", axis=1, tiled=True),
    )
    hidden_part, cot_part = (
        lax.all_to_all(full_hidden, "section", split_axis=1, concat_axis=0, tiled=True),
        lax.all_to_all(full_cot, "section", split_axis=1, concat_axis=0, tiled=True),
    )
    partial_value = lax.dot_general(
        hidden_part, slab, (((1,), (1,)), ((), ())), preferred_element_type=jnp.float32
    )
    columns = lax.axis_index("vocab") * rows_here + jnp.arange(rows_here, dtype=jnp.int32)
    raw_logits = lax.psum_scatter(partial_value, "section", scatter_dimension=0, tiled=True)
    capped, exp_logits, target_hit, local_total, local_pick = local_parts(
        raw_logits, target_ids, columns
    )
    exp_total, picked = lax.psum((local_total, local_pick), "vocab")
    token_loss, dlogit = finish(capped, exp_logits, target_hit, exp_total, picked, loss_grad)
    all_ids = lax.all_gather(token_ids, "section", axis=0, tiled=True)
    all_dlogit = lax.all_gather(dlogit, "section", axis=0, tiled=True)
    total_tokens = all_dlogit.shape[0]
    blocks = shards // sections
    narrow = share_width // sections
    arranged_slab = slab.reshape(rows_here, blocks, sections, narrow)
    term = jnp.einsum(
        "tv,vkrw->trkw", all_dlogit, arranged_slab, preferred_element_type=jnp.float32
    )
    term = term.reshape(total_tokens, shards * narrow)
    piece = lax.psum_scatter(term, "vocab", scatter_dimension=1, tiled=True).astype(jnp.bfloat16)
    slots = lax.all_to_all(piece, "section", split_axis=0, concat_axis=0, tiled=True).reshape(
        sections, own_tokens, narrow
    )
    base_bit = blocks.bit_length() - 1
    rank_high = lax.axis_index("vocab") // blocks
    for level in range(sections.bit_length() - 1):
        span = 1 << level
        shaped = slots.reshape(sections // (2 * span), 2, span, own_tokens, narrow)
        mine_bit = rank_high // span % 2
        lower = shaped[:, 0]
        upper = shaped[:, 1]
        keep = jnp.where(mine_bit == 0, lower, upper)
        outgoing = jnp.where(mine_bit == 0, upper, lower)
        incoming = from_partner(outgoing, "vocab", base_bit + level)
        first = jnp.where(mine_bit == 0, keep, incoming)
        second = jnp.where(mine_bit == 0, incoming, keep)
        slots = jnp.stack([first, second], axis=1).reshape(sections, own_tokens, narrow)
    hidden_grad = jnp.transpose(slots, (1, 0, 2)).reshape(own_tokens, sections * narrow)
    onehot = (all_ids[:, None] == columns[None, :]).astype(jnp.bfloat16)
    embed_scale = math.sqrt(model_width)
    tied_grad = left_product(all_dlogit, hidden_part) + left_product(onehot, cot_part) * embed_scale
    return (token_loss, hidden_grad, tied_grad.astype(jnp.bfloat16))


def on_device(hidden, slab, token_ids, target_ids, input_cot, loss_grad):
    sections = lax.axis_size("section")
    shards = lax.axis_size("vocab")
    fits = (
        sections == 4
        and shards == 2 * sections
        and hidden.shape[0] % 128 == 0
        and slab.shape[0] % 256 == 0
    )
    step = fused if fits else general
    return step(hidden, slab, token_ids, target_ids, input_cot, loss_grad)


def solution(mesh):
    placed = (
        P("section", "vocab"),
        P("vocab", "section"),
        P("section"),
        P("section"),
        P("section", "vocab"),
        P("section"),
    )
    return jax.shard_map(
        on_device,
        mesh=mesh,
        in_specs=placed,
        out_specs=(P("section"), P("section", "vocab"), P("vocab", "section")),
        check_vma=False,
    )
```

profile of v0, /device:TPU:6, one launch (start us, length us, event | category | flops | bytes accessed | tf_op | source)
XLA Modules:
  0.0 101.2 jit_solution(16574993596236946074)
XLA Ops:
  0.6 0.0 copy-start
  0.6 0.9 copy-done
  1.5 0.0 copy-start.1
  1.5 0.9 copy-done.1
  2.5 0.0 copy-start.2
  2.5 0.7 copy-done.2
  3.1 0.0 copy-start.3
  3.1 0.7 copy-done.3
  3.8 0.0 copy-start.4
  3.8 0.7 copy-done.4
  4.4 94.6 %fused.1 = (f32[1,128]{1,0:T(1,128)S(1)}, bf16[576,128]{1,0:T(8,128)(2,1)S(1)}, bf16[2048,1152]{1,0:T(8,128)(2,1)S(1)}) custom-call(bf16[576,128]{1,0:T(8,128)(2,1)S(1)} %bitcast.7, bf16[576,128]{1,0:T(8,128)(2,1)S(1)} %bitcast.8, bf16[2048,1152]{1,0:T(8,128)(2,1)} %slab_hbm.1, s32[1,128]{1,0:T(1,128)S(1)} %bitcast.9, s32[1,128]{1,0:T(1,128)S(1)} %bitcast.10, ...), custom_call_target="tpu_custom_call" | custom-call | tf_op jit(solution)/shard_map/fused/pallas_call | solution.py:447
  99.0 2.2 %put_out.1 = (f32[1,128]{1,0:T(1,128)}, bf16[576,128]{1,0:T(8,128)(2,1)}, bf16[2048,1152]{1,0:T(8,128)(2,1)}) custom-call(f32[1,128]{1,0:T(1,128)S(1)} %get-tuple-element.9.loss, bf16[576,128]{1,0:T(8,128)(2,1)S(1)} %get-tuple-element.10.hgrad, bf16[2048,1152]{1,0:T(8,128)(2,1)S(1)} %get-tuple-element.11.tied), custom_call_target="tpu_custom_call" | custom-call | tf_op jit(solution)/shard_map/put_out/pallas_call | solution.py:465
Async XLA Ops:
  0.6 0.9 copy-start
  1.5 0.9 copy-start.1
  2.5 0.7 copy-start.2
  3.1 0.7 copy-start.3
  3.8 0.7 copy-start.4
where the time goes:
time: 101 us
  Pallas kernels  96.8 us (96%)
  local copies, waits for them, and re-layouts  3.78 us (4%)
    pallas_call x1, Pallas kernels, fused(): pl.pallas_call(functools.partial(fused_kernel, (S, V)), out_shape=(jax.Sh...  94.6 us
    unnamed x10, local copies, waits for them, and re-layouts  3.78 us
    pallas_call x1, Pallas kernels, fused(): pl.pallas_call(put_out, out_shape=tuple((jax.ShapeDtypeStruct(x.shape, x....  2.24 us

commit v1 on v0

--- a/solution.py
+++ b/solution.py
@@ -218,17 +218,17 @@
     relay(nx, high)
     logit_send(5, nx, 0, high, nx)
 
-    @pl.when(z != s)
-    def _():
-        for r in range(S):
-            t = (s + r) % S
-            got(cq.at[t], cz_r.at[t])
-            forward(cq.at[t], t)
-
-    for t in range(S):
-        got(cm.at[t], cm_r.at[t])
-        assemble(cf, cq, cm, t)
-
+    apart = jnp.abs(z - s)
+
+    def pass_cot(distance):
+        @pl.when(apart == distance)
+        def _():
+            for r in range(S):
+                t = (s + r) % S
+                got(cq.at[t], cz_r.at[t])
+                forward(cq.at[t], t)
+
+    pass_cot(1)
     logit_got(2, 1, high)
     logit_got(3, 0, low)
     logit_got(4, 1, low)
@@ -259,6 +259,7 @@
     for r in range(1, V):
         rc(stat_tx, stat_rx.at[v], st_s.at[r - 1], st_r.at[v], (s, (v + r) % V)).start()
     stat_rx[v] = stat_tx[...]
+    pass_cot(2)
     for r in range(1, V):
         u = (v + r) % V
         got(stat_rx.at[u], st_r.at[u])
@@ -333,11 +334,19 @@
     grad_got(4, far, low)
     grad_got(5, far, high)
     term(far)
-    pass_on(far, False)
-    for r in range(1, S):
-        q = s ^ r
+
+    def fin_pass(q):
         got(zr.at[q], g_r.at[q])
         fin_send(q, zr.at[q])
+
+    fin_pass(nx)
+    fin_pass(ny)
+    pass_on(far, False)
+    for distance in range(3, Z):
+        pass_cot(distance)
+    for t in range(S):
+        got(cm.at[t], cm_r.at[t])
+        assemble(cf, cq, cm, t)
 
     for r in range(1, S):
         t = (s + r) % S
@@ -356,7 +365,10 @@
         tied[rows, :] = (head + embed * root).astype(bf16)
         return carry
 
-    lax.fori_loop(0, R // tile, tied_tile, 0)
+    middle = R // tile // 2
+    lax.fori_loop(0, middle, tied_tile, 0)
+    fin_pass(far)
+    lax.fori_loop(middle, R // tile, tied_tile, 0)
 
     for r in range(1, Z):
         u = (z + r) % Z
@@ -444,6 +456,7 @@
     ]
     block = pl.BlockSpec(memory_space=vm)
     anywhere = pl.BlockSpec(memory_space=pl.ANY)
+    far_memory = pl.BlockSpec(memory_space=pltpu.HBM)
     results = pl.pallas_call(
         functools.partial(fused_kernel, (S, V)),
         out_shape=(
@@ -451,7 +464,7 @@
             jax.ShapeDtypeStruct((W, T), bf16),
             jax.ShapeDtypeStruct((R, Q), bf16),
         ),
-        in_specs=[anywhere] * 6,
+        in_specs=[far_memory] * 6,
         out_specs=(block, block, block),
         scratch_shapes=scratch,
         compiler_params=pltpu.CompilerParams(
@@ -459,8 +472,13 @@
         ),
         name="fused",
     )(
-        hidden.T, input_cot.T, slab,
-        token_ids.reshape(1, T), target_ids.reshape(1, T), loss_grad.reshape(1, T),
+        *(
+            pltpu.with_memory_space_constraint(x, pltpu.HBM)
+            for x in (
+                hidden.T, input_cot.T, slab,
+                token_ids.reshape(1, T), target_ids.reshape(1, T), loss_grad.reshape(1, T),
+            )
+        )
     )
     loss, hgrad, tied = pl.pallas_call(
         put_out,

time: 101 us -> 93.4 us (0.925)
  Pallas kernels: 96.8 us -> 92.6 us
  local copies, waits for them, and re-layouts: 3.78 us -> 0 us
    pallas_call x1, Pallas kernels: 94.6 us -> 90.4 us  [fused(): pl.pallas_call(functools.partial(fused_kernel, (S, V)), out_shape=(jax.Sh...]
    unnamed x10 -> x0, local copies, waits for them, and re-layouts: 3.78 us -> none
where the time goes in v1:
time: 93.4 us; the launch traced here: 93.3 us
  Pallas kernels  92.6 us (99%)
    pallas_call x1, Pallas kernels, fused(): pl.pallas_call(functools.partial(fused_kernel, (S, V)), out_shape=(jax.Sh...  90.4 us
    pallas_call x1, Pallas kernels, fused(): pl.pallas_call(put_out, out_shape=tuple((jax.ShapeDtypeStruct(x.shape, x....  2.24 us

profile of v1, /device:TPU:6, one launch (start us, length us, event | category | flops | bytes accessed | tf_op | source)
XLA Modules:
  0.0 93.3 jit_solution(16082812190156657147)
XLA Ops:
  0.6 90.4 %fused.1 = (f32[1,128]{1,0:T(1,128)S(1)}, bf16[576,128]{1,0:T(8,128)(2,1)S(1)}, bf16[2048,1152]{1,0:T(8,128)(2,1)S(1)}) custom-call(bf16[576,128]{1,0:T(8,128)(2,1)} %bitcast.7, bf16[576,128]{1,0:T(8,128)(2,1)} %bitcast.8, bf16[2048,1152]{1,0:T(8,128)(2,1)} %slab_hbm.1, s32[1,128]{1,0:T(1,128)} %bitcast.9, s32[1,128]{1,0:T(1,128)} %bitcast.10, f32[1,128]{1,0:T(1,128)} %bitcast.11), custom_call_target="tpu_custom_call" | custom-call | tf_op jit(solution)/shard_map/fused/pallas_call | solution.py:460
  91.0 2.2 %put_out.1 = (f32[1,128]{1,0:T(1,128)}, bf16[576,128]{1,0:T(8,128)(2,1)}, bf16[2048,1152]{1,0:T(8,128)(2,1)}) custom-call(f32[1,128]{1,0:T(1,128)S(1)} %get-tuple-element.9.loss, bf16[576,128]{1,0:T(8,128)(2,1)S(1)} %get-tuple-element.10.hgrad, bf16[2048,1152]{1,0:T(8,128)(2,1)S(1)} %get-tuple-element.11.tied), custom_call_target="tpu_custom_call" | custom-call | tf_op jit(solution)/shard_map/put_out/pallas_call | solution.py:483

commit v2 on v1

--- a/solution.py
+++ b/solution.py
@@ -15,6 +15,10 @@
 bf16 = jnp.bfloat16
 
 
+steps = 2
+shares = 2
+
+
 def encode(x):
     y = x / (jnp.abs(x) + code_knee) * code_top
     return jnp.floor(y + 0.5).astype(jnp.int32).astype(jnp.int16)
@@ -34,16 +38,17 @@
 def fused_kernel(
     dims, hid_hbm, cot_hbm, slab_hbm, tok_hbm, tgt_hbm, scale_hbm, loss, hgrad, tied,
     hid, cot, tok, tgt, scale,
-    slab, zg, hq, hm, h, snd, rcv, own, cq, cm, cf, ids, tid_tx, cap, ex, stat_tx, stat_rx,
-    dl, gt, px_rx, gs, zr, fin,
+    slab, zg, hq, hm, h, snd, rcv, own, cq, cm, cf, ids, tid_tx, cd, stat_tx, stat_rx,
+    info, dl, gt, px_rx, gs, zr, fin,
     in_sem, zr_s, zr_r, zl_s, zl_r, pl_s, pl_r, mt_s, mt_r, cp_s, cp_r, cr_s, cl_s, cz_r,
-    cm_s, cm_r, id_s, id_r, rs_s, rs_r, st_s, st_r, ag_s, ag_r, px_s, px_r, g_s, g_r, f_s, f_r,
+    cm_s, cm_r, id_s, id_r, in_s, in_r, rs_s, rs_r, st_s, st_r, ag_s, ag_r, px_s, px_r, g_s, g_r, f_s, f_r,
 ):
     S, V = dims
     Z = V // 2
     W, T = hid.shape
     R, Q = slab.shape
-    half = R // 2
+    span = R // steps
+    half = span // 2
     s = lax.axis_index("section")
     v = lax.axis_index("vocab")
     z = v // 2
@@ -80,35 +85,48 @@
         pl.semaphore_signal(bar, inc=1, device_id=(s, (v + r) % V), device_id_type=pl.DeviceIdType.MESH)
     for load in loads[:5]:
         load.wait()
-    tid_tx[...] = jnp.broadcast_to(tok[...], tid_tx.shape)
-    ids[s] = jnp.broadcast_to(tok[...], tid_tx.shape)
+    both_ids = jnp.concatenate([jnp.broadcast_to(x[...], (4, T)) for x in (tok, tgt)], axis=0)
+    tid_tx[...] = both_ids
+    ids[s] = both_ids
     pl.semaphore_wait(bar, S + V - 2)
 
-    def z_send(k):
+    piece = W // shares
+    slices = [slice(f * piece, (f + 1) * piece) for f in range(shares)]
+
+    def z_send(k, f):
+        part = slices[f]
+        n = k * shares + f
         b = z - k
 
         @pl.when((z < Z - 1) & (b >= 0))
         def _():
-            rc(hid if k == 0 else zg.at[b], zg.at[b], zr_s.at[k], zr_r.at[k], (s, v + 2)).start()
+            src = hid.at[part] if k == 0 else zg.at[b, part]
+            rc(src, zg.at[b, part], zr_s.at[n], zr_r.at[n], (s, v + 2)).start()
 
         d = z + k
 
         @pl.when((z > 0) & (d <= Z - 1))
         def _():
-            rc(hid if k == 0 else zg.at[d], zg.at[d], zl_s.at[k], zl_r.at[k], (s, v - 2)).start()
-
-    def plane_send(b, src):
+            src = hid.at[part] if k == 0 else zg.at[d, part]
+            rc(src, zg.at[d, part], zl_s.at[n], zl_r.at[n], (s, v - 2)).start()
+
+    def plane_send(b, src, f):
+        part = slices[f]
+
         @pl.when(b != s)
         def _():
-            rc(src, hq.at[s], pl_s.at[b], pl_r.at[s], (b, v)).start()
+            rc(src, hq.at[s, part], pl_s.at[b * shares + f], pl_r.at[s * shares + f], (b, v)).start()
 
         @pl.when(b == s)
         def _():
-            rc(src, hm.at[s], mt_s.at[s], mt_r.at[s], (s, mate)).start()
-            hq[s] = src[...]
-
-    z_send(0)
-    plane_send(z, hid)
+            n = s * shares + f
+            rc(src, hm.at[s, part], mt_s.at[n], mt_r.at[n], (s, mate)).start()
+            hq[s, part] = src[...]
+
+    for f in range(shares):
+        z_send(0, f)
+    for f in range(shares):
+        plane_send(z, hid.at[slices[f]], f)
 
     @pl.when(s != z)
     def _():
@@ -121,40 +139,28 @@
     for k in range(Z - 1):
         b = z - 1 - k
         d = z + 1 + k
-
-        @pl.when(b >= 0)
-        def _():
-            got(zg.at[b], zr_r.at[k])
-
-        @pl.when(d <= Z - 1)
-        def _():
-            got(zg.at[d], zl_r.at[k])
-
-        if k + 1 < Z - 1:
-            z_send(k + 1)
-
-        @pl.when(b >= 0)
-        def _():
-            plane_send(b, zg.at[b])
-
-        @pl.when(d <= Z - 1)
-        def _():
-            plane_send(d, zg.at[d])
-
-    for r in range(1, S):
-        t = (s + r) % S
-        got(hq.at[t], pl_r.at[t])
-        rc(hq.at[t], hm.at[t], mt_s.at[t], mt_r.at[t], (s, mate)).start()
-
-    def assemble(full, mine, other, t):
-        cols = slice(t % 2 * T, (t % 2 + 1) * T)
-        full[t // 2, pl.ds(pl.multiple_of(c * W, 16), W), cols] = mine[t]
-        full[t // 2, pl.ds(pl.multiple_of((1 - c) * W, 16), W), cols] = other[t]
-
-    for t in range(S):
-        got(hm.at[t], mt_r.at[t])
-        assemble(h, hq, hm, t)
-    loads[5].wait()
+        for f in range(shares):
+            part = slices[f]
+            n = k * shares + f
+
+            @pl.when(b >= 0)
+            def _():
+                got(zg.at[b, part], zr_r.at[n])
+
+            @pl.when(d <= Z - 1)
+            def _():
+                got(zg.at[d, part], zl_r.at[n])
+
+            if k + 1 < Z - 1:
+                z_send(k + 1, f)
+
+            @pl.when(b >= 0)
+            def _():
+                plane_send(b, zg.at[b, part], f)
+
+            @pl.when(d <= Z - 1)
+            def _():
+                plane_send(d, zg.at[d, part], f)
 
     def forward(src, t):
         @pl.when((z >= s) & (z < Z - 1))
@@ -176,19 +182,51 @@
             got(cq.at[t], cp_r.at[t])
             forward(cq.at[t], t)
 
-    low, high = slice(0, half), slice(half, R)
-
-    def logits(p, last):
+    apart = jnp.abs(z - s)
+
+    def pass_cot(distance, first, last):
+        @pl.when(apart == distance)
+        def _():
+            for r in range(first, last):
+                t = (s + r) % S
+                got(cq.at[t], cz_r.at[t])
+                forward(cq.at[t], t)
+
+    for f in range(shares):
+        for r in range(1, S):
+            t = s ^ r
+            n = t * shares + f
+            got(hq.at[t, slices[f]], pl_r.at[n])
+            rc(hq.at[t, slices[f]], hm.at[t, slices[f]], mt_s.at[n], mt_r.at[n], (s, mate)).start()
+
+    def assemble(full, mine, other, t):
+        cols = slice(t % 2 * T, (t % 2 + 1) * T)
+        full[t // 2, pl.ds(pl.multiple_of(c * W, 16), W), cols] = mine[t]
+        full[t // 2, pl.ds(pl.multiple_of((1 - c) * W, 16), W), cols] = other[t]
+
+    for t in range(S):
+        for f in range(shares):
+            got(hm.at[t, slices[f]], mt_r.at[t * shares + f])
+        assemble(h, hq, hm, t)
+    loads[5].wait()
+
+    low = [slice(k * span, k * span + half) for k in range(steps)]
+    high = [slice(k * span + half, (k + 1) * span) for k in range(steps)]
+    other = 1 - s // 2
+    even = s % 2 == 0
+
+    def logits(k):
         def logit_tile(j, carry):
-            rows = pl.ds(pl.multiple_of(j * tile, tile), tile)
-            part = jnp.dot(slab[rows, :], h[p], preferred_element_type=f32)
+            rows = pl.ds(pl.multiple_of(k * span + j * tile, tile), tile)
+            part = jnp.dot(slab[rows, :], h[other], preferred_element_type=f32)
             for m in range(2):
-                snd[2 * p + m, rows, :] = encode(part[:, m * T:(m + 1) * T])
-            if last:
-                own[rows, :] = jnp.where(s % 2 == 0, part[:, :T], part[:, T:])
+                snd[2 * other + m, rows, :] = encode(part[:, m * T:(m + 1) * T])
+            part = jnp.dot(slab[rows, :], h[s // 2], preferred_element_type=f32)
+            own[rows, :] = jnp.where(even, part[:, :T], part[:, T:])
+            snd[nx, rows, :] = encode(jnp.where(even, part[:, T:], part[:, :T]))
             return carry
 
-        lax.fori_loop(0, R // tile, logit_tile, 0)
+        lax.fori_loop(0, span // tile, logit_tile, 0)
 
     def logit_send(n, t, slot, part, to):
         rc(snd.at[t, part], rcv.at[slot, part], rs_s.at[n], rs_r.at[n], (to, v)).start()
@@ -204,62 +242,110 @@
 
         lax.fori_loop(0, half // tile, relay_tile, 0)
 
-    other = 1 - s // 2
-    logits(other, False)
-    logit_send(0, far, 2, low, nx)
-    logit_send(1, far, 2, high, ny)
-    logit_send(2, ny, 1, high, ny)
-    logits(s // 2, True)
-    logit_send(3, nx, 0, low, nx)
-    logit_got(0, 2, low)
-    relay(ny, low)
-    logit_send(4, ny, 1, low, ny)
-    logit_got(1, 2, high)
-    relay(nx, high)
-    logit_send(5, nx, 0, high, nx)
-
-    apart = jnp.abs(z - s)
-
-    def pass_cot(distance):
-        @pl.when(apart == distance)
-        def _():
-            for r in range(S):
-                t = (s + r) % S
-                got(cq.at[t], cz_r.at[t])
-                forward(cq.at[t], t)
-
-    pass_cot(1)
-    logit_got(2, 1, high)
-    logit_got(3, 0, low)
-    logit_got(4, 1, low)
-    logit_got(5, 0, high)
+    def logit_start(k):
+        logit_send(6 * k, far, 2, low[k], nx)
+        logit_send(6 * k + 1, far, 2, high[k], ny)
+        logit_send(6 * k + 2, nx, 0, low[k], nx)
+        logit_send(6 * k + 3, ny, 1, high[k], ny)
+
+    def logit_relay(k):
+        logit_got(6 * k, 2, low[k])
+        relay(ny, low[k])
+        logit_send(6 * k + 4, ny, 1, low[k], ny)
+        logit_got(6 * k + 1, 2, high[k])
+        relay(nx, high[k])
+        logit_send(6 * k + 5, nx, 0, high[k], nx)
+
     soft = 128
     target = tgt[...]
+    unit = logit_cap / code_top
 
     def row_ids(j, n, width):
         return v * R + j * n + lax.broadcasted_iota(jnp.int32, (n, width), 0)
 
-    def soft_tile(j, carry):
-        total, pick = carry
-        rows = pl.ds(pl.multiple_of(j * soft, soft), soft)
-        raw = own[rows, :] + decode(rcv[0, rows, :]) + decode(rcv[1, rows, :])
-        capped = logit_cap * jnp.tanh(raw / logit_cap)
-        e = jnp.exp(capped)
-        cap[rows, :] = capped
-        ex[rows, :] = e
-        hit = row_ids(j, soft, T) == target
-        total = total + jnp.sum(e, axis=0, keepdims=True)
-        pick = pick + jnp.sum(jnp.where(hit, capped, 0.0), axis=0, keepdims=True)
-        return total, pick
+    def softmax_sums(k, sums):
+        logit_got(6 * k + 2, 0, low[k])
+        logit_got(6 * k + 3, 1, high[k])
+        logit_got(6 * k + 4, 1, low[k])
+        logit_got(6 * k + 5, 0, high[k])
+
+        def soft_tile(j, carry):
+            total, pick = carry
+            rows = pl.ds(pl.multiple_of(j * soft, soft), soft)
+            raw = own[rows, :] + decode(rcv[0, rows, :]) + decode(rcv[1, rows, :])
+            bent = jnp.tanh(raw / logit_cap)
+            code = jnp.floor(bent * code_top + 0.5)
+            cd[s, rows, :] = code.astype(jnp.int32).astype(jnp.int16)
+            hit = row_ids(j, soft, T) == target
+            total = total + jnp.sum(jnp.exp(code * unit), axis=0, keepdims=True)
+            pick = pick + jnp.sum(jnp.where(hit, logit_cap * bent, 0.0), axis=0, keepdims=True)
+            return total, pick
+
+        count = span // soft
+        return lax.fori_loop(k * count, (k + 1) * count, soft_tile, sums)
+
+    def code_send(n, t, part, to):
+        block = cd.at[t, part]
+        rc(block, block, ag_s.at[n], ag_r.at[n], (to, v)).start()
+
+    def code_got(n, t, part):
+        got(cd.at[t, part], ag_r.at[n])
+
+    def code_start(k):
+        code_send(6 * k, s, high[k], nx)
+        code_send(6 * k + 1, s, low[k], ny)
+        code_send(6 * k + 2, s, low[k], nx)
+        code_send(6 * k + 3, s, high[k], ny)
+
+    def code_relay(k):
+        code_got(6 * k + 1, ny, low[k])
+        code_send(6 * k + 4, ny, low[k], nx)
+        code_got(6 * k, nx, high[k])
+        code_send(6 * k + 5, nx, high[k], ny)
+
+    def info_got(t):
+        got(info.at[t], in_r.at[t])
+
+    def grad(t, k):
+        scale_row = info[t][0:1, :]
+        gain_row = info[t][1:2, :]
+        target_row = ids[t][4:5, :]
+
+        def grad_tile(j, carry):
+            rows = pl.ds(pl.multiple_of(j * soft, soft), soft)
+            code = cd[t, rows, :].astype(jnp.int32).astype(f32)
+            hit = row_ids(j, soft, T) == target_row
+            slope = 1.0 - (code * (1.0 / code_top)) ** 2
+            away = jnp.exp(code * unit) * scale_row - jnp.where(hit, gain_row, 0.0)
+            dl[t, rows, :] = (away * slope).astype(bf16)
+            return carry
+
+        count = span // soft
+        lax.fori_loop(k * count, (k + 1) * count, grad_tile, 0)
 
     zero = jnp.zeros((1, T), f32)
-    total, pick = lax.fori_loop(0, R // soft, soft_tile, (zero, zero))
+    logits(0)
+    logit_start(0)
+    logits(1)
+    pass_cot(1, 0, 2)
+    logit_relay(0)
+    logit_start(1)
+    pass_cot(1, 2, S)
+    pass_cot(2, 0, 2)
+    sums = softmax_sums(0, (zero, zero))
+    pass_cot(2, 2, S)
+    logit_relay(1)
+    code_start(0)
+    total, pick = softmax_sums(1, sums)
     stat_tx[0:8, :] = jnp.broadcast_to(total, (8, T))
     stat_tx[8:16, :] = jnp.broadcast_to(pick, (8, T))
     for r in range(1, V):
         rc(stat_tx, stat_rx.at[v], st_s.at[r - 1], st_r.at[v], (s, (v + r) % V)).start()
     stat_rx[v] = stat_tx[...]
-    pass_cot(2)
+    for r in range(1, S):
+        t = (s + r) % S
+        got(ids.at[t], id_r.at[t])
+    code_relay(0)
     for r in range(1, V):
         u = (v + r) % V
         got(stat_rx.at[u], st_r.at[u])
@@ -269,28 +355,13 @@
     total = sums[0:1, :]
     loss[...] = jnp.log(total) - sums[8:9, :]
     gain = scale[...]
-
-    def grad_tile(j, carry):
-        rows = pl.ds(pl.multiple_of(j * soft, soft), soft)
-        capped = cap[rows, :]
-        hit = (row_ids(j, soft, T) == target).astype(f32)
-        slope = 1.0 - (capped / logit_cap) ** 2
-        dl[s, rows, :] = (gain * (ex[rows, :] / total - hit) * slope).astype(bf16)
-        return carry
-
-    lax.fori_loop(0, R // soft, grad_tile, 0)
-
-    def grad_send(n, t, part, to):
-        block = dl.at[t, part]
-        rc(block, block, ag_s.at[n], ag_r.at[n], (to, v)).start()
-
-    def grad_got(n, t, part):
-        got(dl.at[t, part], ag_r.at[n])
-
-    grad_send(0, s, high, nx)
-    grad_send(1, s, low, ny)
-    grad_send(2, s, low, nx)
-    grad_send(3, s, high, ny)
+    info[s] = jnp.concatenate(
+        [gain / total, jnp.broadcast_to(gain, (7, T))], axis=0
+    )
+    for r in range(1, S):
+        t = s ^ r
+        rc(info.at[s], info.at[s], in_s.at[r - 1], in_r.at[s], (t, v)).start()
+    code_start(1)
 
     def term(t):
         g = lax.dot_general(
@@ -319,38 +390,43 @@
         else:
             rc(gs.at[t], zr.at[s], g_s.at[t], g_r.at[s], (t, v)).start()
 
+    for k in range(steps):
+        grad(s, k)
     term(s)
-    grad_got(1, ny, low)
-    grad_send(4, ny, low, nx)
-    grad_got(0, nx, high)
-    grad_send(5, nx, high, ny)
+    for t, n in ((nx, 2), (ny, 3)):
+        info_got(t)
+    code_got(2, nx, low[0])
+    grad(nx, 0)
     pass_on(s, True)
-    grad_got(2, nx, low)
+    code_got(3, ny, high[0])
+    grad(ny, 0)
+    code_relay(1)
+    info_got(far)
+    code_got(4, far, low[0])
+    code_got(5, far, high[0])
+    grad(far, 0)
+    code_got(8, nx, low[1])
+    grad(nx, 1)
     term(nx)
-    grad_got(3, ny, high)
+    code_got(9, ny, high[1])
+    grad(ny, 1)
     term(ny)
     pass_on(nx, False)
     pass_on(ny, False)
-    grad_got(4, far, low)
-    grad_got(5, far, high)
+    code_got(10, far, low[1])
+    code_got(11, far, high[1])
+    grad(far, 1)
     term(far)
 
     def fin_pass(q):
         got(zr.at[q], g_r.at[q])
         fin_send(q, zr.at[q])
 
-    fin_pass(nx)
-    fin_pass(ny)
-    pass_on(far, False)
     for distance in range(3, Z):
-        pass_cot(distance)
+        pass_cot(distance, 0, S)
     for t in range(S):
         got(cm.at[t], cm_r.at[t])
         assemble(cf, cq, cm, t)
-
-    for r in range(1, S):
-        t = (s + r) % S
-        got(ids.at[t], id_r.at[t])
     every = jnp.concatenate([ids[t][0:1, :] for t in range(S)], axis=1)
     root = math.sqrt(Q * S)
 
@@ -365,11 +441,16 @@
         tied[rows, :] = (head + embed * root).astype(bf16)
         return carry
 
-    middle = R // tile // 2
-    lax.fori_loop(0, middle, tied_tile, 0)
+    tiles = R // tile
+    marks = [0, tiles // 8, tiles // 4, tiles * 5 // 8, tiles]
+    lax.fori_loop(marks[0], marks[1], tied_tile, 0)
+    pass_on(far, False)
+    lax.fori_loop(marks[1], marks[2], tied_tile, 0)
+    fin_pass(nx)
+    fin_pass(ny)
+    lax.fori_loop(marks[2], marks[3], tied_tile, 0)
     fin_pass(far)
-    lax.fori_loop(middle, R // tile, tied_tile, 0)
-
+    lax.fori_loop(marks[3], marks[4], tied_tile, 0)
     for r in range(1, Z):
         u = (z + r) % Z
         got(fin.at[u], f_r.at[u])
@@ -379,19 +460,22 @@
     hgrad[...] = acc.astype(bf16)
 
     for k in range(Z - 1):
-        @pl.when((z < Z - 1) & (z - k >= 0))
-        def _():
-            sent(hid, zr_s.at[k])
-
-        @pl.when((z > 0) & (z + k <= Z - 1))
-        def _():
-            sent(hid, zl_s.at[k])
+        for f in range(shares):
+            @pl.when((z < Z - 1) & (z - k >= 0))
+            def _():
+                sent(hid.at[slices[f]], zr_s.at[k * shares + f])
+
+            @pl.when((z > 0) & (z + k <= Z - 1))
+            def _():
+                sent(hid.at[slices[f]], zl_s.at[k * shares + f])
     for b in range(S):
         @pl.when(b != s)
         def _():
-            sent(hid, pl_s.at[b])
+            for f in range(shares):
+                sent(hid.at[slices[f]], pl_s.at[b * shares + f])
             sent(gs.at[b], g_s.at[b])
-        sent(hid, mt_s.at[b])
+        for f in range(shares):
+            sent(hid.at[slices[f]], mt_s.at[b * shares + f])
         sent(cot, cm_s.at[b])
         sent(px_rx.at[b], px_s.at[b])
 
@@ -412,9 +496,10 @@
         sent(cot, cp_s)
     for r in range(1, S):
         sent(tid_tx, id_s.at[r - 1])
-    for n in range(6):
-        sent(snd.at[0, low], rs_s.at[n])
-        sent(dl.at[0, low], ag_s.at[n])
+        sent(info.at[0], in_s.at[r - 1])
+    for n in range(6 * steps):
+        sent(snd.at[0, low[0]], rs_s.at[n])
+        sent(cd.at[0, low[0]], ag_s.at[n])
     for r in range(1, V):
         sent(stat_tx, st_s.at[r - 1])
 
@@ -446,12 +531,13 @@
         vm((R, Q), bf16), half, half, half, both,
         vm((S, R, T), jnp.int16), vm((3, R, T), jnp.int16), vm((R, T), f32),
         half, half, both, vm((S, 8, T), jnp.int32), vm((8, T), jnp.int32),
-        vm((R, T), f32), vm((R, T), f32), vm((16, T), f32), vm((V, 16, T), f32),
-        vm((S, R, T), bf16), vm((S, Q, T), f32), vm((S, W, T), f32), half, half, vm((Z, W, T), bf16),
-        dma((6,)), dma((Z,)), dma((Z,)), dma((Z,)), dma((Z,)),
-        dma((S,)), dma((S,)), dma((S,)), dma((S,)), dma, dma((S,)),
+        vm((S, R, T), jnp.int16), vm((16, T), f32), vm((V, 16, T), f32),
+        vm((S, 8, T), f32), vm((S, R, T), bf16), vm((S, Q, T), f32), vm((S, W, T), f32), half, half, vm((Z, W, T), bf16),
+        dma((6,)), *[dma((Z * shares,))] * 4,
+        *[dma((S * shares,))] * 4, dma, dma((S,)),
         dma((S,)), dma((S,)), dma((S,)), dma((S,)), dma((S,)), dma((S,)), dma((S,)),
-        dma((6,)), dma((6,)), dma((V,)), dma((V,)), dma((6,)), dma((6,)),
+        dma((S,)), dma((S,)),
+        dma((6 * steps,)), dma((6 * steps,)), dma((V,)), dma((V,)), dma((6 * steps,)), dma((6 * steps,)),
         dma((S,)), dma((S,)), dma((S,)), dma((S,)), dma((Z,)), dma((Z,)),
     ]
     block = pl.BlockSpec(memory_space=vm)
@@ -594,7 +680,8 @@
         sections == 4
         and shards == 2 * sections
         and hidden.shape[0] % 128 == 0
-        and slab.shape[0] % 256 == 0
+        and slab.shape[0] % 2048 == 0
+        and hidden.shape[1] % 32 == 0
     )
     step = fused if fits else general
     return step(hidden, slab, token_ids, target_ids, input_cot, loss_grad)

time: 93.4 us -> 84.1 us (0.900)
  Pallas kernels: 92.6 us -> 83.3 us
    pallas_call x1, Pallas kernels: 90.4 us -> 81.1 us  [fused(): pl.pallas_call(functools.partial(fused_kernel, (S, V)), out_shape=(jax.Sh...]
where the time goes in v2:
time: 84.1 us; the launch traced here: 84 us
  Pallas kernels  83.3 us (99%)
    pallas_call x1, Pallas kernels, fused(): pl.pallas_call(functools.partial(fused_kernel, (S, V)), out_shape=(jax.Sh...  81.1 us
    pallas_call x1, Pallas kernels, fused(): pl.pallas_call(put_out, out_shape=tuple((jax.ShapeDtypeStruct(x.shape, x....  2.24 us

profile of v2, /device:TPU:6, one launch (start us, length us, event | category | flops | bytes accessed | tf_op | source)
XLA Modules:
  0.0 84.0 jit_solution(15945119576893503267)
XLA Ops:
  0.6 81.1 %fused.1 = (f32[1,128]{1,0:T(1,128)S(1)}, bf16[576,128]{1,0:T(8,128)(2,1)S(1)}, bf16[2048,1152]{1,0:T(8,128)(2,1)S(1)}) custom-call(bf16[576,128]{1,0:T(8,128)(2,1)} %bitcast.7, bf16[576,128]{1,0:T(8,128)(2,1)} %bitcast.8, bf16[2048,1152]{1,0:T(8,128)(2,1)} %slab_hbm.1, s32[1,128]{1,0:T(1,128)} %bitcast.9, s32[1,128]{1,0:T(1,128)} %bitcast.10, f32[1,128]{1,0:T(1,128)} %bitcast.11), custom_call_target="tpu_custom_call" | custom-call | tf_op jit(solution)/shard_map/fused/pallas_call | solution.py:546
  81.7 2.2 %put_out.1 = (f32[1,128]{1,0:T(1,128)}, bf16[576,128]{1,0:T(8,128)(2,1)}, bf16[2048,1152]{1,0:T(8,128)(2,1)}) custom-call(f32[1,128]{1,0:T(1,128)S(1)} %get-tuple-element.9.loss, bf16[576,128]{1,0:T(8,128)(2,1)S(1)} %get-tuple-element.10.hgrad, bf16[2048,1152]{1,0:T(8,128)(2,1)S(1)} %get-tuple-element.11.tied), custom_call_target="tpu_custom_call" | custom-call | tf_op jit(solution)/shard_map/put_out/pallas_call | solution.py:569

commit v3 on v2

--- a/solution.py
+++ b/solution.py
@@ -15,7 +15,7 @@
 bf16 = jnp.bfloat16
 
 
-steps = 2
+steps = 4
 shares = 2
 
 
@@ -39,9 +39,9 @@
     dims, hid_hbm, cot_hbm, slab_hbm, tok_hbm, tgt_hbm, scale_hbm, loss, hgrad, tied,
     hid, cot, tok, tgt, scale,
     slab, zg, hq, hm, h, snd, rcv, own, cq, cm, cf, ids, tid_tx, cd, stat_tx, stat_rx,
-    info, dl, gt, px_rx, gs, zr, fin,
+    info, dl, gp, gt, px_rx, gs, zr, fin, zf, zsum, whole,
     in_sem, zr_s, zr_r, zl_s, zl_r, pl_s, pl_r, mt_s, mt_r, cp_s, cp_r, cr_s, cl_s, cz_r,
-    cm_s, cm_r, id_s, id_r, in_s, in_r, rs_s, rs_r, st_s, st_r, ag_s, ag_r, px_s, px_r, g_s, g_r, f_s, f_r,
+    cm_s, cm_r, id_s, id_r, in_s, in_r, rs_s, rs_r, st_s, st_r, ag_s, ag_r, px_s, px_r, g_s, g_r, f_s, f_r, zf_s, zf_r, zw_s, zw_r,
 ):
     S, V = dims
     Z = V // 2
@@ -324,19 +324,24 @@
         lax.fori_loop(k * count, (k + 1) * count, grad_tile, 0)
 
     zero = jnp.zeros((1, T), f32)
-    logits(0)
-    logit_start(0)
-    logits(1)
+    sums = (zero, zero)
+    for k in range(steps):
+        logits(k)
+        logit_start(k)
+        if k:
+            logit_relay(k - 1)
     pass_cot(1, 0, 2)
-    logit_relay(0)
-    logit_start(1)
+    sums = softmax_sums(0, sums)
+    for k in range(1, steps - 2):
+        sums = softmax_sums(k, sums)
+    logit_relay(steps - 1)
     pass_cot(1, 2, S)
+    for k in range(steps - 2):
+        code_start(k)
     pass_cot(2, 0, 2)
-    sums = softmax_sums(0, (zero, zero))
-    pass_cot(2, 2, S)
-    logit_relay(1)
-    code_start(0)
-    total, pick = softmax_sums(1, sums)
+    sums = softmax_sums(steps - 2, sums)
+    code_start(steps - 2)
+    total, pick = softmax_sums(steps - 1, sums)
     stat_tx[0:8, :] = jnp.broadcast_to(total, (8, T))
     stat_tx[8:16, :] = jnp.broadcast_to(pick, (8, T))
     for r in range(1, V):
@@ -346,6 +351,7 @@
         t = (s + r) % S
         got(ids.at[t], id_r.at[t])
     code_relay(0)
+    pass_cot(2, 2, S)
     for r in range(1, V):
         u = (v + r) % V
         got(stat_rx.at[u], st_r.at[u])
@@ -361,72 +367,152 @@
     for r in range(1, S):
         t = s ^ r
         rc(info.at[s], info.at[s], in_s.at[r - 1], in_r.at[s], (t, v)).start()
-    code_start(1)
+    code_start(steps - 1)
+
+    def rows_term(t, part):
+        return lax.dot_general(
+            dl[t, part], slab[part], (((0,), (0,)), ((), ())), preferred_element_type=f32
+        )
+
+    def give(t, g):
+        gt[t] = g.T
+        block = gt.at[t, pl.ds(pl.multiple_of((1 - c) * W, 16), W)]
+        rc(block, px_rx.at[t], px_s.at[t], px_r.at[t], (s, mate)).start()
 
     def term(t):
-        g = lax.dot_general(
-            dl[t], slab[...], (((0,), (0,)), ((), ())), preferred_element_type=f32
-        )
-
-        gt[t] = g.T
-        give = gt.at[t, pl.ds(pl.multiple_of((1 - c) * W, 16), W)]
-        rc(give, px_rx.at[t], px_s.at[t], px_r.at[t], (s, mate)).start()
-
-    def fin_send(q, src):
+        give(t, rows_term(t, slice(0, R)))
+
+    lead, rest = slice(0, W // 2), slice(W // 2, W)
+
+    def fin_send(q, src, part):
         @pl.when(q != z)
         def _():
-            rc(src, fin.at[z], f_s.at[q], f_r.at[z], (s, 2 * q + c)).start()
+            rc(src, fin.at[z, part], f_s.at[q], f_r.at[z], (s, 2 * q + c)).start()
 
         @pl.when(q == z)
         def _():
-            fin[z] = src[...]
-
-    def pass_on(t, local):
+            fin[z, part] = src[...]
+
+    def pass_on(t):
         got(px_rx.at[t], px_r.at[t])
         kept = gt[t, pl.ds(pl.multiple_of(c * W, 16), W), :]
         gs[t] = (kept + px_rx[t]).astype(bf16)
-        if local:
-            fin_send(s, gs.at[t])
-        else:
-            rc(gs.at[t], zr.at[s], g_s.at[t], g_r.at[s], (t, v)).start()
+
+    def pass_near(t):
+        pass_on(t)
+        rc(gs.at[t], zr.at[s], g_s.at[t], g_r.at[s], (t, v)).start()
+
+    def pass_far():
+        pass_on(far)
+
+        @pl.when(z != s)
+        def _():
+            rc(gs.at[far, rest], zf.at[z], zf_s, zf_r.at[z], (s, 2 * s + c)).start()
+
+        @pl.when(z == s)
+        def _():
+            zf[z] = gs[far, rest]
+
+        rc(gs.at[far, lead], zr.at[s, lead], g_s.at[far], g_r.at[s], (far, v)).start()
+
+    def gather_far():
+        @pl.when(z == s)
+        def _():
+            for r in range(1, Z):
+                u = (z + r) % Z
+                got(zf.at[u], zf_r.at[u])
+            acc = zf[0].astype(f32)
+            for u in range(1, Z):
+                acc = acc + zf[u].astype(f32)
+            zsum[...] = acc.astype(bf16)
+            rc(zsum, whole, zw_s, zw_r, (far, v)).start()
 
     for k in range(steps):
         grad(s, k)
     term(s)
-    for t, n in ((nx, 2), (ny, 3)):
+    code_relay(1)
+    for t in (nx, ny):
         info_got(t)
-    code_got(2, nx, low[0])
-    grad(nx, 0)
-    pass_on(s, True)
-    code_got(3, ny, high[0])
-    grad(ny, 0)
-    code_relay(1)
+
+    def near_got(k):
+        code_got(6 * k + 2, nx, low[k])
+        code_got(6 * k + 3, ny, high[k])
+        grad(nx, k)
+        grad(ny, k)
+
+    def far_got(k):
+        code_got(6 * k + 4, far, low[k])
+        code_got(6 * k + 5, far, high[k])
+        grad(far, k)
+
+    near_got(0)
+    pass_on(s)
+    fin_send(s, gs.at[s], slice(0, W))
+    near_got(1)
+    code_relay(2)
+    near_got(2)
     info_got(far)
-    code_got(4, far, low[0])
-    code_got(5, far, high[0])
-    grad(far, 0)
-    code_got(8, nx, low[1])
-    grad(nx, 1)
+    far_got(0)
+    code_relay(3)
+    code_got(20, nx, low[3])
+    grad(nx, 3)
     term(nx)
-    code_got(9, ny, high[1])
-    grad(ny, 1)
+    code_got(21, ny, high[3])
+    grad(ny, 3)
     term(ny)
-    pass_on(nx, False)
-    pass_on(ny, False)
-    code_got(10, far, low[1])
-    code_got(11, far, high[1])
-    grad(far, 1)
-    term(far)
-
-    def fin_pass(q):
-        got(zr.at[q], g_r.at[q])
-        fin_send(q, zr.at[q])
-
-    for distance in range(3, Z):
-        pass_cot(distance, 0, S)
-    for t in range(S):
-        got(cm.at[t], cm_r.at[t])
-        assemble(cf, cq, cm, t)
+    far_got(1)
+    far_got(2)
+    pass_near(nx)
+    early = slice(0, (steps - 1) * span)
+    gp[...] = rows_term(far, early)
+    pass_near(ny)
+    far_got(3)
+    give(far, gp[...] + rows_term(far, slice(early.stop, R)))
+
+    def drain():
+        for k in range(Z - 1):
+            for f in range(shares):
+                @pl.when((z < Z - 1) & (z - k >= 0))
+                def _():
+                    sent(hid.at[slices[f]], zr_s.at[k * shares + f])
+
+                @pl.when((z > 0) & (z + k <= Z - 1))
+                def _():
+                    sent(hid.at[slices[f]], zl_s.at[k * shares + f])
+        for b in range(S):
+            @pl.when(b != s)
+            def _():
+                for f in range(shares):
+                    sent(hid.at[slices[f]], pl_s.at[b * shares + f])
+            for f in range(shares):
+                sent(hid.at[slices[f]], mt_s.at[b * shares + f])
+            sent(cot, cm_s.at[b])
+            sent(px_rx.at[b], px_s.at[b])
+
+            @pl.when((z >= s) & (z < Z - 1))
+            def _():
+                sent(cot, cr_s.at[b])
+
+            @pl.when((z <= s) & (z > 0))
+            def _():
+                sent(cot, cl_s.at[b])
+
+        @pl.when(s != z)
+        def _():
+            sent(cot, cp_s)
+        for r in range(1, S):
+            sent(tid_tx, id_s.at[r - 1])
+            sent(info.at[0], in_s.at[r - 1])
+        for n in range(6 * steps):
+            sent(snd.at[0, low[0]], rs_s.at[n])
+            sent(cd.at[0, low[0]], ag_s.at[n])
+        for r in range(1, V):
+            sent(stat_tx, st_s.at[r - 1])
+
+    def fin_pass(q, part):
+        got(zr.at[q, part], g_r.at[q])
+        fin_send(q, zr.at[q, part], part)
+
     every = jnp.concatenate([ids[t][0:1, :] for t in range(S)], axis=1)
     root = math.sqrt(Q * S)
 
@@ -442,73 +528,67 @@
         return carry
 
     tiles = R // tile
-    marks = [0, tiles // 8, tiles // 4, tiles * 5 // 8, tiles]
+    marks = [0, tiles // 8, tiles // 2, tiles]
+    pass_far()
+    for distance in range(3, Z):
+        pass_cot(distance, 0, S)
+    for t in range(S):
+        got(cm.at[t], cm_r.at[t])
+        assemble(cf, cq, cm, t)
     lax.fori_loop(marks[0], marks[1], tied_tile, 0)
-    pass_on(far, False)
+    drain()
+    fin_pass(nx, slice(0, W))
+    fin_pass(ny, slice(0, W))
+    fin_pass(far, lead)
     lax.fori_loop(marks[1], marks[2], tied_tile, 0)
-    fin_pass(nx)
-    fin_pass(ny)
+    gather_far()
     lax.fori_loop(marks[2], marks[3], tied_tile, 0)
-    fin_pass(far)
-    lax.fori_loop(marks[3], marks[4], tied_tile, 0)
-    for r in range(1, Z):
-        u = (z + r) % Z
-        got(fin.at[u], f_r.at[u])
-    acc = fin[0].astype(f32)
-    for u in range(1, Z):
-        acc = acc + fin[u].astype(f32)
-    hgrad[...] = acc.astype(bf16)
-
-    for k in range(Z - 1):
-        for f in range(shares):
-            @pl.when((z < Z - 1) & (z - k >= 0))
-            def _():
-                sent(hid.at[slices[f]], zr_s.at[k * shares + f])
-
-            @pl.when((z > 0) & (z + k <= Z - 1))
-            def _():
-                sent(hid.at[slices[f]], zl_s.at[k * shares + f])
-    for b in range(S):
-        @pl.when(b != s)
-        def _():
-            for f in range(shares):
-                sent(hid.at[slices[f]], pl_s.at[b * shares + f])
-            sent(gs.at[b], g_s.at[b])
-        for f in range(shares):
-            sent(hid.at[slices[f]], mt_s.at[b * shares + f])
-        sent(cot, cm_s.at[b])
-        sent(px_rx.at[b], px_s.at[b])
-
-        @pl.when((z >= s) & (z < Z - 1))
-        def _():
-            sent(cot, cr_s.at[b])
-
-        @pl.when((z <= s) & (z > 0))
-        def _():
-            sent(cot, cl_s.at[b])
-    for q in range(Z):
-        @pl.when(q != z)
-        def _():
-            sent(gs.at[0], f_s.at[q])
-
-    @pl.when(s != z)
+
+    def fin_sum(part):
+        for r in range(1, Z):
+            u = (z + r) % Z
+            got(fin.at[u, part], f_r.at[u])
+        acc = fin[0, part].astype(f32)
+        for u in range(1, Z):
+            acc = acc + fin[u, part].astype(f32)
+        hgrad[part] = acc.astype(bf16)
+
+    @pl.when(z == far)
     def _():
-        sent(cot, cp_s)
+        fin_sum(lead)
+        got(whole, zw_r)
+        hgrad[rest] = whole[...]
+
+    @pl.when(z != far)
+    def _():
+        fin_sum(slice(0, W))
+
+
     for r in range(1, S):
-        sent(tid_tx, id_s.at[r - 1])
-        sent(info.at[0], in_s.at[r - 1])
-    for n in range(6 * steps):
-        sent(snd.at[0, low[0]], rs_s.at[n])
-        sent(cd.at[0, low[0]], ag_s.at[n])
-    for r in range(1, V):
-        sent(stat_tx, st_s.at[r - 1])
+        part = lead if r == 3 else slice(0, W)
+        sent(gs.at[0, part], g_s.at[s ^ r])
+    for r in range(S):
+        part = lead if r == 3 else slice(0, W)
+
+        @pl.when(s ^ r != z)
+        def _():
+            sent(gs.at[0, part], f_s.at[s ^ r])
+
+    @pl.when(z != s)
+    def _():
+        sent(gs.at[0, rest], zf_s)
+
+    @pl.when(z == s)
+    def _():
+        sent(zsum, zw_s)
 
 
 def put_out(loss, hgrad, tied, loss_out, hgrad_out, tied_out, sems):
-    moves = [
-        pltpu.make_async_copy(src, dst, sems.at[i])
-        for i, (src, dst) in enumerate(((tied, tied_out), (hgrad, hgrad_out), (loss, loss_out)))
-    ]
+    count = sems.shape[0] - 2
+    rows = tied.shape[0] // count
+    pairs = [(tied.at[pl.ds(n * rows, rows)], tied_out.at[pl.ds(n * rows, rows)]) for n in range(count)]
+    pairs += [(hgrad, hgrad_out), (loss, loss_out)]
+    moves = [pltpu.make_async_copy(src, dst, sems.at[i]) for i, (src, dst) in enumerate(pairs)]
     for move in moves:
         move.start()
     for move in moves:
@@ -532,13 +612,15 @@
         vm((S, R, T), jnp.int16), vm((3, R, T), jnp.int16), vm((R, T), f32),
         half, half, both, vm((S, 8, T), jnp.int32), vm((8, T), jnp.int32),
         vm((S, R, T), jnp.int16), vm((16, T), f32), vm((V, 16, T), f32),
-        vm((S, 8, T), f32), vm((S, R, T), bf16), vm((S, Q, T), f32), vm((S, W, T), f32), half, half, vm((Z, W, T), bf16),
+        vm((S, 8, T), f32), vm((S, R, T), bf16), vm((T, Q), f32), vm((S, Q, T), f32), vm((S, W, T), f32), half, half, vm((Z, W, T), bf16),
+        vm((Z, W // 2, T), bf16), vm((W // 2, T), bf16), vm((W // 2, T), bf16),
         dma((6,)), *[dma((Z * shares,))] * 4,
         *[dma((S * shares,))] * 4, dma, dma((S,)),
         dma((S,)), dma((S,)), dma((S,)), dma((S,)), dma((S,)), dma((S,)), dma((S,)),
         dma((S,)), dma((S,)),
         dma((6 * steps,)), dma((6 * steps,)), dma((V,)), dma((V,)), dma((6 * steps,)), dma((6 * steps,)),
         dma((S,)), dma((S,)), dma((S,)), dma((S,)), dma((Z,)), dma((Z,)),
+        dma, dma((Z,)), dma, dma,
     ]
     block = pl.BlockSpec(memory_space=vm)
     anywhere = pl.BlockSpec(memory_space=pl.ANY)
@@ -571,7 +653,7 @@
         out_shape=tuple(jax.ShapeDtypeStruct(x.shape, x.dtype) for x in results),
         in_specs=[block] * 3,
         out_specs=(anywhere,) * 3,
-        scratch_shapes=[dma((3,))],
+        scratch_shapes=[dma((10,))],
         compiler_params=pltpu.CompilerParams(vmem_limit_bytes=8 * 2**20),
         name="put_out",
     )(*results)

time: 84.1 us -> 80.4 us (0.956)
  Pallas kernels: 83.3 us -> 79.6 us
    pallas_call x1, Pallas kernels: 81.1 us -> 77.3 us  [fused(): pl.pallas_call(functools.partial(fused_kernel, (S, V)), out_shape=(jax.Sh...]
where the time goes in v3:
time: 80.4 us; the launch traced here: 80.3 us
  Pallas kernels  79.6 us (99%)
    pallas_call x1, Pallas kernels, fused(): pl.pallas_call(functools.partial(fused_kernel, (S, V)), out_shape=(jax.Sh...  77.3 us
    pallas_call x1, Pallas kernels, fused(): pl.pallas_call(put_out, out_shape=tuple((jax.ShapeDtypeStruct(x.shape, x....  2.3 us

profile of v3, /device:TPU:6, one launch (start us, length us, event | category | flops | bytes accessed | tf_op | source)
XLA Modules:
  0.0 80.3 jit_solution(2845562091728966668)
XLA Ops:
  0.6 77.3 %fused.1 = (f32[1,128]{1,0:T(1,128)S(1)}, bf16[576,128]{1,0:T(8,128)(2,1)S(1)}, bf16[2048,1152]{1,0:T(8,128)(2,1)S(1)}) custom-call(bf16[576,128]{1,0:T(8,128)(2,1)} %bitcast.7, bf16[576,128]{1,0:T(8,128)(2,1)} %bitcast.8, bf16[2048,1152]{1,0:T(8,128)(2,1)} %slab_hbm.1, s32[1,128]{1,0:T(1,128)} %bitcast.9, s32[1,128]{1,0:T(1,128)} %bitcast.10, f32[1,128]{1,0:T(1,128)} %bitcast.11), custom_call_target="tpu_custom_call" | custom-call | tf_op jit(solution)/shard_map/fused/pallas_call | solution.py:628
  78.0 2.3 %put_out.1 = (f32[1,128]{1,0:T(1,128)}, bf16[576,128]{1,0:T(8,128)(2,1)}, bf16[2048,1152]{1,0:T(8,128)(2,1)}) custom-call(f32[1,128]{1,0:T(1,128)S(1)} %get-tuple-element.9.loss, bf16[576,128]{1,0:T(8,128)(2,1)S(1)} %get-tuple-element.10.hgrad, bf16[2048,1152]{1,0:T(8,128)(2,1)S(1)} %get-tuple-element.11.tied), custom_call_target="tpu_custom_call" | custom-call | tf_op jit(solution)/shard_map/put_out/pallas_call | solution.py:651

commit v4 on v3

--- a/solution.py
+++ b/solution.py
@@ -39,7 +39,7 @@
     dims, hid_hbm, cot_hbm, slab_hbm, tok_hbm, tgt_hbm, scale_hbm, loss, hgrad, tied,
     hid, cot, tok, tgt, scale,
     slab, zg, hq, hm, h, snd, rcv, own, cq, cm, cf, ids, tid_tx, cd, stat_tx, stat_rx,
-    info, dl, gp, gt, px_rx, gs, zr, fin, zf, zsum, whole,
+    info, dl, gp, gt, px_rx, gs, zr, fin, zf, zsum, whole, emb,
     in_sem, zr_s, zr_r, zl_s, zl_r, pl_s, pl_r, mt_s, mt_r, cp_s, cp_r, cr_s, cl_s, cz_r,
     cm_s, cm_r, id_s, id_r, in_s, in_r, rs_s, rs_r, st_s, st_r, ag_s, ag_r, px_s, px_r, g_s, g_r, f_s, f_r, zf_s, zf_r, zw_s, zw_r,
 ):
@@ -115,12 +115,12 @@
 
         @pl.when(b != s)
         def _():
-            rc(src, hq.at[s, part], pl_s.at[b * shares + f], pl_r.at[s * shares + f], (b, v)).start()
+            rc(src, hq.at[s, part], pl_s, pl_r.at[s * shares + f], (b, v)).start()
 
         @pl.when(b == s)
         def _():
             n = s * shares + f
-            rc(src, hm.at[s, part], mt_s.at[n], mt_r.at[n], (s, mate)).start()
+            rc(src, hm.at[s, part], mt_s, mt_r.at[n], (s, mate)).start()
             hq[s, part] = src[...]
 
     for f in range(shares):
@@ -134,7 +134,7 @@
 
     for r in range(1, S):
         t = (s + r) % S
-        rc(tid_tx, ids.at[s], id_s.at[r - 1], id_r.at[s], (t, v)).start()
+        rc(tid_tx, ids.at[s], id_s, id_r.at[s], (t, v)).start()
 
     for k in range(Z - 1):
         b = z - 1 - k
@@ -171,7 +171,7 @@
         def _():
             rc(src, cq.at[t], cl_s.at[t], cz_r.at[t], (s, v - 2)).start()
 
-        rc(src, cm.at[t], cm_s.at[t], cm_r.at[t], (s, mate)).start()
+        rc(src, cm.at[t], cm_s, cm_r.at[t], (s, mate)).start()
 
     @pl.when(z == s)
     def _():
@@ -197,7 +197,7 @@
             t = s ^ r
             n = t * shares + f
             got(hq.at[t, slices[f]], pl_r.at[n])
-            rc(hq.at[t, slices[f]], hm.at[t, slices[f]], mt_s.at[n], mt_r.at[n], (s, mate)).start()
+            rc(hq.at[t, slices[f]], hm.at[t, slices[f]], mt_s, mt_r.at[n], (s, mate)).start()
 
     def assemble(full, mine, other, t):
         cols = slice(t % 2 * T, (t % 2 + 1) * T)
@@ -229,7 +229,7 @@
         lax.fori_loop(0, span // tile, logit_tile, 0)
 
     def logit_send(n, t, slot, part, to):
-        rc(snd.at[t, part], rcv.at[slot, part], rs_s.at[n], rs_r.at[n], (to, v)).start()
+        rc(snd.at[t, part], rcv.at[slot, part], rs_s, rs_r.at[n], (to, v)).start()
 
     def logit_got(n, slot, part):
         got(rcv.at[slot, part], rs_r.at[n])
@@ -243,18 +243,18 @@
         lax.fori_loop(0, half // tile, relay_tile, 0)
 
     def logit_start(k):
-        logit_send(6 * k, far, 2, low[k], nx)
-        logit_send(6 * k + 1, far, 2, high[k], ny)
-        logit_send(6 * k + 2, nx, 0, low[k], nx)
-        logit_send(6 * k + 3, ny, 1, high[k], ny)
+        logit_send(3 * k, far, 2, low[k], nx)
+        logit_send(3 * k + 1, far, 2, high[k], ny)
+        logit_send(3 * k + 2, nx, 0, low[k], nx)
+        logit_send(3 * k + 2, ny, 1, high[k], ny)
 
     def logit_relay(k):
-        logit_got(6 * k, 2, low[k])
+        logit_got(3 * k, 2, low[k])
         relay(ny, low[k])
-        logit_send(6 * k + 4, ny, 1, low[k], ny)
-        logit_got(6 * k + 1, 2, high[k])
+        logit_send(3 * k + 2, ny, 1, low[k], ny)
+        logit_got(3 * k + 1, 2, high[k])
         relay(nx, high[k])
-        logit_send(6 * k + 5, nx, 0, high[k], nx)
+        logit_send(3 * k + 2, nx, 0, high[k], nx)
 
     soft = 128
     target = tgt[...]
@@ -264,10 +264,7 @@
         return v * R + j * n + lax.broadcasted_iota(jnp.int32, (n, width), 0)
 
     def softmax_sums(k, sums):
-        logit_got(6 * k + 2, 0, low[k])
-        logit_got(6 * k + 3, 1, high[k])
-        logit_got(6 * k + 4, 1, low[k])
-        logit_got(6 * k + 5, 0, high[k])
+        logit_got(3 * k + 2, slice(0, 2), slice(k * span, (k + 1) * span))
 
         def soft_tile(j, carry):
             total, pick = carry
@@ -286,22 +283,22 @@
 
     def code_send(n, t, part, to):
         block = cd.at[t, part]
-        rc(block, block, ag_s.at[n], ag_r.at[n], (to, v)).start()
+        rc(block, block, ag_s, ag_r.at[n], (to, v)).start()
 
     def code_got(n, t, part):
         got(cd.at[t, part], ag_r.at[n])
 
     def code_start(k):
-        code_send(6 * k, s, high[k], nx)
-        code_send(6 * k + 1, s, low[k], ny)
-        code_send(6 * k + 2, s, low[k], nx)
-        code_send(6 * k + 3, s, high[k], ny)
+        code_send(5 * k, s, high[k], nx)
+        code_send(5 * k + 1, s, low[k], ny)
+        code_send(5 * k + 2, s, low[k], nx)
+        code_send(5 * k + 3, s, high[k], ny)
 
     def code_relay(k):
-        code_got(6 * k + 1, ny, low[k])
-        code_send(6 * k + 4, ny, low[k], nx)
-        code_got(6 * k, nx, high[k])
-        code_send(6 * k + 5, nx, high[k], ny)
+        code_got(5 * k + 1, ny, low[k])
+        code_send(5 * k + 4, ny, low[k], nx)
+        code_got(5 * k, nx, high[k])
+        code_send(5 * k + 4, nx, high[k], ny)
 
     def info_got(t):
         got(info.at[t], in_r.at[t])
@@ -323,6 +320,26 @@
         count = span // soft
         lax.fori_loop(k * count, (k + 1) * count, grad_tile, 0)
 
+    root = math.sqrt(Q * S)
+
+    def embed_tile(j, carry):
+        rows = pl.ds(pl.multiple_of(j * tile, tile), tile)
+        every = jnp.concatenate([ids[t][0:1, :] for t in range(S)], axis=1)
+        onehot = (row_ids(j, tile, S * T) == every).astype(f32).astype(bf16)
+        embed = 0.0
+        for p in range(S // 2):
+            embed = embed + over_tokens(onehot[:, 2 * p * T:2 * (p + 1) * T], cf[p])
+        emb[rows, :] = embed * root
+        return carry
+
+    def embed_ready():
+        for t in range(S):
+            got(cm.at[t], cm_r.at[t])
+            assemble(cf, cq, cm, t)
+
+    tiles = R // tile
+    close = apart < 3
+
     zero = jnp.zeros((1, T), f32)
     sums = (zero, zero)
     for k in range(steps):
@@ -330,28 +347,36 @@
         logit_start(k)
         if k:
             logit_relay(k - 1)
-    pass_cot(1, 0, 2)
+        if k == 1:
+            pass_cot(1, 0, 2)
+        if k == 2:
+            pass_cot(1, 2, S)
+    pass_cot(2, 0, 2)
     sums = softmax_sums(0, sums)
     for k in range(1, steps - 2):
         sums = softmax_sums(k, sums)
     logit_relay(steps - 1)
-    pass_cot(1, 2, S)
     for k in range(steps - 2):
         code_start(k)
-    pass_cot(2, 0, 2)
+    pass_cot(2, 2, S)
     sums = softmax_sums(steps - 2, sums)
     code_start(steps - 2)
     total, pick = softmax_sums(steps - 1, sums)
     stat_tx[0:8, :] = jnp.broadcast_to(total, (8, T))
     stat_tx[8:16, :] = jnp.broadcast_to(pick, (8, T))
     for r in range(1, V):
-        rc(stat_tx, stat_rx.at[v], st_s.at[r - 1], st_r.at[v], (s, (v + r) % V)).start()
+        rc(stat_tx, stat_rx.at[v], st_s, st_r.at[v], (s, (v + r) % V)).start()
     stat_rx[v] = stat_tx[...]
     for r in range(1, S):
         t = (s + r) % S
         got(ids.at[t], id_r.at[t])
     code_relay(0)
-    pass_cot(2, 2, S)
+
+    @pl.when(close)
+    def _():
+        embed_ready()
+        lax.fori_loop(0, tiles // 2, embed_tile, 0)
+
     for r in range(1, V):
         u = (v + r) % V
         got(stat_rx.at[u], st_r.at[u])
@@ -366,7 +391,7 @@
     )
     for r in range(1, S):
         t = s ^ r
-        rc(info.at[s], info.at[s], in_s.at[r - 1], in_r.at[s], (t, v)).start()
+        rc(info.at[s], info.at[s], in_s, in_r.at[s], (t, v)).start()
     code_start(steps - 1)
 
     def rows_term(t, part):
@@ -377,7 +402,7 @@
     def give(t, g):
         gt[t] = g.T
         block = gt.at[t, pl.ds(pl.multiple_of((1 - c) * W, 16), W)]
-        rc(block, px_rx.at[t], px_s.at[t], px_r.at[t], (s, mate)).start()
+        rc(block, px_rx.at[t], px_s, px_r.at[t], (s, mate)).start()
 
     def term(t):
         give(t, rows_term(t, slice(0, R)))
@@ -430,20 +455,31 @@
     for k in range(steps):
         grad(s, k)
     term(s)
+    @pl.when(close)
+    def _():
+        lax.fori_loop(tiles // 2, tiles, embed_tile, 0)
+
     code_relay(1)
     for t in (nx, ny):
         info_got(t)
 
     def near_got(k):
-        code_got(6 * k + 2, nx, low[k])
-        code_got(6 * k + 3, ny, high[k])
+        code_got(5 * k + 2, nx, low[k])
+        code_got(5 * k + 3, ny, high[k])
         grad(nx, k)
         grad(ny, k)
 
     def far_got(k):
-        code_got(6 * k + 4, far, low[k])
-        code_got(6 * k + 5, far, high[k])
+        code_got(5 * k + 4, far, slice(k * span, (k + 1) * span))
         grad(far, k)
+
+    early, late = slice(0, (steps - 1) * span), slice((steps - 1) * span, R)
+
+    def early_term(t, slot):
+        gp[slot] = rows_term(t, early)
+
+    def late_term(t, slot):
+        give(t, gp[slot] + rows_term(t, late))
 
     near_got(0)
     pass_on(s)
@@ -451,23 +487,21 @@
     near_got(1)
     code_relay(2)
     near_got(2)
+    code_relay(3)
     info_got(far)
+    early_term(nx, 0)
+    early_term(ny, 1)
+    near_got(3)
+    late_term(nx, 0)
+    late_term(ny, 1)
     far_got(0)
-    code_relay(3)
-    code_got(20, nx, low[3])
-    grad(nx, 3)
-    term(nx)
-    code_got(21, ny, high[3])
-    grad(ny, 3)
-    term(ny)
     far_got(1)
+    pass_near(nx)
     far_got(2)
-    pass_near(nx)
-    early = slice(0, (steps - 1) * span)
-    gp[...] = rows_term(far, early)
     pass_near(ny)
+    early_term(far, 2)
     far_got(3)
-    give(far, gp[...] + rows_term(far, slice(early.stop, R)))
+    late_term(far, 2)
 
     def drain():
         for k in range(Z - 1):
@@ -479,16 +513,9 @@
                 @pl.when((z > 0) & (z + k <= Z - 1))
                 def _():
                     sent(hid.at[slices[f]], zl_s.at[k * shares + f])
+        sent(hq.at[0:S - 1], pl_s)
+        sent(hq, mt_s)
         for b in range(S):
-            @pl.when(b != s)
-            def _():
-                for f in range(shares):
-                    sent(hid.at[slices[f]], pl_s.at[b * shares + f])
-            for f in range(shares):
-                sent(hid.at[slices[f]], mt_s.at[b * shares + f])
-            sent(cot, cm_s.at[b])
-            sent(px_rx.at[b], px_s.at[b])
-
             @pl.when((z >= s) & (z < Z - 1))
             def _():
                 sent(cot, cr_s.at[b])
@@ -500,49 +527,49 @@
         @pl.when(s != z)
         def _():
             sent(cot, cp_s)
-        for r in range(1, S):
-            sent(tid_tx, id_s.at[r - 1])
-            sent(info.at[0], in_s.at[r - 1])
-        for n in range(6 * steps):
-            sent(snd.at[0, low[0]], rs_s.at[n])
-            sent(cd.at[0, low[0]], ag_s.at[n])
-        for r in range(1, V):
-            sent(stat_tx, st_s.at[r - 1])
+        sent(ids.at[0:S - 1], id_s)
+        sent(info.at[0:S - 1], in_s)
+        sent(rcv, rs_s)
+        sent(cd.at[0:S - 1], ag_s)
+        sent(stat_rx.at[0:V - 1], st_s)
 
     def fin_pass(q, part):
         got(zr.at[q, part], g_r.at[q])
         fin_send(q, zr.at[q, part], part)
 
-    every = jnp.concatenate([ids[t][0:1, :] for t in range(S)], axis=1)
-    root = math.sqrt(Q * S)
-
     def tied_tile(j, carry):
         rows = pl.ds(pl.multiple_of(j * tile, tile), tile)
-        onehot = (row_ids(j, tile, S * T) == every).astype(f32).astype(bf16)
-        head, embed = 0.0, 0.0
+        head = emb[rows, :]
         for p in range(S // 2):
             lhs = jnp.concatenate([dl[2 * p, rows, :], dl[2 * p + 1, rows, :]], axis=1)
             head = head + over_tokens(lhs, h[p])
-            embed = embed + over_tokens(onehot[:, 2 * p * T:2 * (p + 1) * T], cf[p])
-        tied[rows, :] = (head + embed * root).astype(bf16)
+        tied[rows, :] = head.astype(bf16)
         return carry
 
-    tiles = R // tile
-    marks = [0, tiles // 8, tiles // 2, tiles]
+    begun = tiles // 4
+    drain()
     pass_far()
-    for distance in range(3, Z):
-        pass_cot(distance, 0, S)
-    for t in range(S):
-        got(cm.at[t], cm_r.at[t])
-        assemble(cf, cq, cm, t)
-    lax.fori_loop(marks[0], marks[1], tied_tile, 0)
-    drain()
+
+    @pl.when(jnp.logical_not(close))
+    def _():
+        for distance in range(3, Z):
+            pass_cot(distance, 0, S)
+        embed_ready()
+
+    def late_embed(first, last):
+        @pl.when(jnp.logical_not(close))
+        def _():
+            lax.fori_loop(first, last, embed_tile, 0)
+
+    late_embed(0, tiles // 4)
     fin_pass(nx, slice(0, W))
+    late_embed(tiles // 4, tiles * 3 // 4)
     fin_pass(ny, slice(0, W))
+    late_embed(tiles * 3 // 4, tiles)
     fin_pass(far, lead)
-    lax.fori_loop(marks[1], marks[2], tied_tile, 0)
+    lax.fori_loop(0, begun, tied_tile, 0)
     gather_far()
-    lax.fori_loop(marks[2], marks[3], tied_tile, 0)
+    lax.fori_loop(begun, tiles, tied_tile, 0)
 
     def fin_sum(part):
         for r in range(1, Z):
@@ -573,6 +600,9 @@
         @pl.when(s ^ r != z)
         def _():
             sent(gs.at[0, part], f_s.at[s ^ r])
+
+    sent(cq, cm_s)
+    sent(px_rx, px_s)
 
     @pl.when(z != s)
     def _():
@@ -612,14 +642,14 @@
         vm((S, R, T), jnp.int16), vm((3, R, T), jnp.int16), vm((R, T), f32),
         half, half, both, vm((S, 8, T), jnp.int32), vm((8, T), jnp.int32),
         vm((S, R, T), jnp.int16), vm((16, T), f32), vm((V, 16, T), f32),
-        vm((S, 8, T), f32), vm((S, R, T), bf16), vm((T, Q), f32), vm((S, Q, T), f32), vm((S, W, T), f32), half, half, vm((Z, W, T), bf16),
-        vm((Z, W // 2, T), bf16), vm((W // 2, T), bf16), vm((W // 2, T), bf16),
+        vm((S, 8, T), f32), vm((S, R, T), bf16), vm((3, T, Q), f32), vm((S, Q, T), f32), vm((S, W, T), f32), half, half, vm((Z, W, T), bf16),
+        vm((Z, W // 2, T), bf16), vm((W // 2, T), bf16), vm((W // 2, T), bf16), vm((R, Q), f32),
         dma((6,)), *[dma((Z * shares,))] * 4,
-        *[dma((S * shares,))] * 4, dma, dma((S,)),
-        dma((S,)), dma((S,)), dma((S,)), dma((S,)), dma((S,)), dma((S,)), dma((S,)),
-        dma((S,)), dma((S,)),
-        dma((6 * steps,)), dma((6 * steps,)), dma((V,)), dma((V,)), dma((6 * steps,)), dma((6 * steps,)),
-        dma((S,)), dma((S,)), dma((S,)), dma((S,)), dma((Z,)), dma((Z,)),
+        dma, dma((S * shares,)), dma, dma((S * shares,)), dma, dma((S,)),
+        dma((S,)), dma((S,)), dma((S,)), dma, dma((S,)), dma, dma((S,)),
+        dma, dma((S,)),
+        dma, dma((3 * steps,)), dma, dma((V,)), dma, dma((5 * steps,)),
+        dma, dma((S,)), dma((S,)), dma((S,)), dma((Z,)), dma((Z,)),
         dma, dma((Z,)), dma, dma,
     ]
     block = pl.BlockSpec(memory_space=vm)

time: 80.4 us -> 77.2 us (0.960)
  Pallas kernels: 79.6 us -> 76.4 us
    pallas_call x1, Pallas kernels: 77.3 us -> 74.1 us  [fused(): pl.pallas_call(functools.partial(fused_kernel, (S, V)), out_shape=(jax.Sh...]
where the time goes in v4:
time: 77.2 us; the launch traced here: 77 us
  Pallas kernels  76.4 us (99%)
    pallas_call x1, Pallas kernels, fused(): pl.pallas_call(functools.partial(fused_kernel, (S, V)), out_shape=(jax.Sh...  74.1 us
    pallas_call x1, Pallas kernels, fused(): pl.pallas_call(put_out, out_shape=tuple((jax.ShapeDtypeStruct(x.shape, x....  2.3 us

profile of v4, /device:TPU:6, one launch (start us, length us, event | category | flops | bytes accessed | tf_op | source)
XLA Modules:
  0.0 77.0 jit_solution(6454553360288649400)
XLA Ops:
  0.6 74.1 %fused.1 = (f32[1,128]{1,0:T(1,128)S(1)}, bf16[576,128]{1,0:T(8,128)(2,1)S(1)}, bf16[2048,1152]{1,0:T(8,128)(2,1)S(1)}) custom-call(bf16[576,128]{1,0:T(8,128)(2,1)} %bitcast.7, bf16[576,128]{1,0:T(8,128)(2,1)} %bitcast.8, bf16[2048,1152]{1,0:T(8,128)(2,1)} %slab_hbm.1, s32[1,128]{1,0:T(1,128)} %bitcast.9, s32[1,128]{1,0:T(1,128)} %bitcast.10, f32[1,128]{1,0:T(1,128)} %bitcast.11), custom_call_target="tpu_custom_call" | custom-call | tf_op jit(solution)/shard_map/fused/pallas_call | solution.py:658
  74.7 2.3 %put_out.1 = (f32[1,128]{1,0:T(1,128)}, bf16[576,128]{1,0:T(8,128)(2,1)}, bf16[2048,1152]{1,0:T(8,128)(2,1)}) custom-call(f32[1,128]{1,0:T(1,128)S(1)} %get-tuple-element.9.loss, bf16[576,128]{1,0:T(8,128)(2,1)S(1)} %get-tuple-element.10.hgrad, bf16[2048,1152]{1,0:T(8,128)(2,1)S(1)} %get-tuple-element.11.tied), custom_call_target="tpu_custom_call" | custom-call | tf_op jit(solution)/shard_map/put_out/pallas_call | solution.py:681

commit v5 on v4

--- a/solution.py
+++ b/solution.py
@@ -15,7 +15,8 @@
 bf16 = jnp.bfloat16
 
 
-steps = 4
+eighths = (0, 1, 2, 4, 6, 8)
+steps = len(eighths) - 1
 shares = 2
 
 
@@ -47,8 +48,8 @@
     Z = V // 2
     W, T = hid.shape
     R, Q = slab.shape
-    span = R // steps
-    half = span // 2
+    edges = [R * n // 8 for n in eighths]
+    spans = [slice(a, b) for a, b in zip(edges, edges[1:])]
     s = lax.axis_index("section")
     v = lax.axis_index("vocab")
     z = v // 2
@@ -210,14 +211,14 @@
         assemble(h, hq, hm, t)
     loads[5].wait()
 
-    low = [slice(k * span, k * span + half) for k in range(steps)]
-    high = [slice(k * span + half, (k + 1) * span) for k in range(steps)]
+    low = [slice(x.start, (x.start + x.stop) // 2) for x in spans]
+    high = [slice((x.start + x.stop) // 2, x.stop) for x in spans]
     other = 1 - s // 2
     even = s % 2 == 0
 
     def logits(k):
         def logit_tile(j, carry):
-            rows = pl.ds(pl.multiple_of(k * span + j * tile, tile), tile)
+            rows = pl.ds(pl.multiple_of(j * tile, tile), tile)
             part = jnp.dot(slab[rows, :], h[other], preferred_element_type=f32)
             for m in range(2):
                 snd[2 * other + m, rows, :] = encode(part[:, m * T:(m + 1) * T])
@@ -226,7 +227,7 @@
             snd[nx, rows, :] = encode(jnp.where(even, part[:, T:], part[:, :T]))
             return carry
 
-        lax.fori_loop(0, span // tile, logit_tile, 0)
+        lax.fori_loop(spans[k].start // tile, spans[k].stop // tile, logit_tile, 0)
 
     def logit_send(n, t, slot, part, to):
         rc(snd.at[t, part], rcv.at[slot, part], rs_s, rs_r.at[n], (to, v)).start()
@@ -236,11 +237,11 @@
 
     def relay(t, part):
         def relay_tile(j, carry):
-            rows = pl.ds(pl.multiple_of(part.start + j * tile, tile), tile)
+            rows = pl.ds(pl.multiple_of(j * soft, soft), soft)
             snd[t, rows, :] = encode(decode(snd[t, rows, :]) + decode(rcv[2, rows, :]))
             return carry
 
-        lax.fori_loop(0, half // tile, relay_tile, 0)
+        lax.fori_loop(part.start // soft, part.stop // soft, relay_tile, 0)
 
     def logit_start(k):
         logit_send(3 * k, far, 2, low[k], nx)
@@ -264,7 +265,7 @@
         return v * R + j * n + lax.broadcasted_iota(jnp.int32, (n, width), 0)
 
     def softmax_sums(k, sums):
-        logit_got(3 * k + 2, slice(0, 2), slice(k * span, (k + 1) * span))
+        logit_got(3 * k + 2, slice(0, 2), spans[k])
 
         def soft_tile(j, carry):
             total, pick = carry
@@ -278,8 +279,7 @@
             pick = pick + jnp.sum(jnp.where(hit, logit_cap * bent, 0.0), axis=0, keepdims=True)
             return total, pick
 
-        count = span // soft
-        return lax.fori_loop(k * count, (k + 1) * count, soft_tile, sums)
+        return lax.fori_loop(spans[k].start // soft, spans[k].stop // soft, soft_tile, sums)
 
     def code_send(n, t, part, to):
         block = cd.at[t, part]
@@ -317,8 +317,7 @@
             dl[t, rows, :] = (away * slope).astype(bf16)
             return carry
 
-        count = span // soft
-        lax.fori_loop(k * count, (k + 1) * count, grad_tile, 0)
+        lax.fori_loop(spans[k].start // soft, spans[k].stop // soft, grad_tile, 0)
 
     root = math.sqrt(Q * S)
 
@@ -345,22 +344,23 @@
     for k in range(steps):
         logits(k)
         logit_start(k)
-        if k:
-            logit_relay(k - 1)
-        if k == 1:
+        if k > 1:
+            logit_relay(k - 2)
+        if k == 3:
             pass_cot(1, 0, 2)
-        if k == 2:
+        if k == 4:
             pass_cot(1, 2, S)
+    logit_relay(steps - 2)
     pass_cot(2, 0, 2)
-    sums = softmax_sums(0, sums)
-    for k in range(1, steps - 2):
+    for k in range(steps // 2):
         sums = softmax_sums(k, sums)
     logit_relay(steps - 1)
-    for k in range(steps - 2):
+    for k in range(steps // 2):
         code_start(k)
     pass_cot(2, 2, S)
-    sums = softmax_sums(steps - 2, sums)
-    code_start(steps - 2)
+    for k in range(steps // 2, steps - 1):
+        sums = softmax_sums(k, sums)
+        code_start(k)
     total, pick = softmax_sums(steps - 1, sums)
     stat_tx[0:8, :] = jnp.broadcast_to(total, (8, T))
     stat_tx[8:16, :] = jnp.broadcast_to(pick, (8, T))
@@ -460,6 +460,7 @@
         lax.fori_loop(tiles // 2, tiles, embed_tile, 0)
 
     code_relay(1)
+    code_relay(2)
     for t in (nx, ny):
         info_got(t)
 
@@ -470,10 +471,10 @@
         grad(ny, k)
 
     def far_got(k):
-        code_got(5 * k + 4, far, slice(k * span, (k + 1) * span))
+        code_got(5 * k + 4, far, spans[k])
         grad(far, k)
 
-    early, late = slice(0, (steps - 1) * span), slice((steps - 1) * span, R)
+    early, late = slice(0, edges[-2]), spans[-1]
 
     def early_term(t, slot):
         gp[slot] = rows_term(t, early)
@@ -484,23 +485,26 @@
     near_got(0)
     pass_on(s)
     fin_send(s, gs.at[s], slice(0, W))
-    near_got(1)
-    code_relay(2)
-    near_got(2)
-    code_relay(3)
+    for k in range(3, steps):
+        near_got(k - 2)
+        code_relay(k)
+    for distance in range(3, Z):
+        pass_cot(distance, 0, S)
     info_got(far)
+    near_got(steps - 2)
     early_term(nx, 0)
     early_term(ny, 1)
-    near_got(3)
+    near_got(steps - 1)
     late_term(nx, 0)
     late_term(ny, 1)
-    far_got(0)
-    far_got(1)
+    for k in range(steps // 2):
+        far_got(k)
     pass_near(nx)
-    far_got(2)
+    for k in range(steps // 2, steps - 1):
+        far_got(k)
     pass_near(ny)
     early_term(far, 2)
-    far_got(3)
+    far_got(steps - 1)
     late_term(far, 2)
 
     def drain():
@@ -552,8 +556,6 @@
 
     @pl.when(jnp.logical_not(close))
     def _():
-        for distance in range(3, Z):
-            pass_cot(distance, 0, S)
         embed_ready()
 
     def late_embed(first, last):

time: 77.2 us -> 76.5 us (level); the launches traced: 77 us -> 75.5 us
  Pallas kernels: 76.4 us -> 74.8 us
    pallas_call x1, Pallas kernels: 74.1 us -> 72.5 us  [fused(): pl.pallas_call(functools.partial(fused_kernel, (S, V)), out_shape=(jax.Sh...]
where the time goes in v5:
time: 76.5 us; the launch traced here: 75.5 us
  Pallas kernels  74.8 us (98%)
    pallas_call x1, Pallas kernels, fused(): pl.pallas_call(functools.partial(fused_kernel, (S, V)), out_shape=(jax.Sh...  72.5 us
    pallas_call x1, Pallas kernels, fused(): pl.pallas_call(put_out, out_shape=tuple((jax.ShapeDtypeStruct(x.shape, x....  2.3 us

profile of v5, /device:TPU:6, one launch (start us, length us, event | category | flops | bytes accessed | tf_op | source)
XLA Modules:
  0.0 75.5 jit_solution(1874520446047332245)
XLA Ops:
  0.6 72.5 %fused.1 = (f32[1,128]{1,0:T(1,128)S(1)}, bf16[576,128]{1,0:T(8,128)(2,1)S(1)}, bf16[2048,1152]{1,0:T(8,128)(2,1)S(1)}) custom-call(bf16[576,128]{1,0:T(8,128)(2,1)} %bitcast.7, bf16[576,128]{1,0:T(8,128)(2,1)} %bitcast.8, bf16[2048,1152]{1,0:T(8,128)(2,1)} %slab_hbm.1, s32[1,128]{1,0:T(1,128)} %bitcast.9, s32[1,128]{1,0:T(1,128)} %bitcast.10, f32[1,128]{1,0:T(1,128)} %bitcast.11), custom_call_target="tpu_custom_call" | custom-call | tf_op jit(solution)/shard_map/fused/pallas_call | solution.py:660
  73.2 2.3 %put_out.1 = (f32[1,128]{1,0:T(1,128)}, bf16[576,128]{1,0:T(8,128)(2,1)}, bf16[2048,1152]{1,0:T(8,128)(2,1)}) custom-call(f32[1,128]{1,0:T(1,128)S(1)} %get-tuple-element.9.loss, bf16[576,128]{1,0:T(8,128)(2,1)S(1)} %get-tuple-element.10.hgrad, bf16[2048,1152]{1,0:T(8,128)(2,1)S(1)} %get-tuple-element.11.tied), custom_call_target="tpu_custom_call" | custom-call | tf_op jit(solution)/shard_map/put_out/pallas_call | solution.py:683

commit v6 on v5

--- a/solution.py
+++ b/solution.py
@@ -135,7 +135,7 @@
 
     for r in range(1, S):
         t = (s + r) % S
-        rc(tid_tx, ids.at[s], id_s, id_r.at[s], (t, v)).start()
+        rc(tid_tx, ids.at[s], id_s, id_r, (t, v)).start()
 
     for k in range(Z - 1):
         b = z - 1 - k
@@ -172,7 +172,7 @@
         def _():
             rc(src, cq.at[t], cl_s.at[t], cz_r.at[t], (s, v - 2)).start()
 
-        rc(src, cm.at[t], cm_s, cm_r.at[t], (s, mate)).start()
+        rc(src, cm.at[t], cm_s, cm_r, (s, mate)).start()
 
     @pl.when(z == s)
     def _():
@@ -332,8 +332,8 @@
         return carry
 
     def embed_ready():
+        got(cm, cm_r)
         for t in range(S):
-            got(cm.at[t], cm_r.at[t])
             assemble(cf, cq, cm, t)
 
     tiles = R // tile
@@ -365,11 +365,9 @@
     stat_tx[0:8, :] = jnp.broadcast_to(total, (8, T))
     stat_tx[8:16, :] = jnp.broadcast_to(pick, (8, T))
     for r in range(1, V):
-        rc(stat_tx, stat_rx.at[v], st_s, st_r.at[v], (s, (v + r) % V)).start()
+        rc(stat_tx, stat_rx.at[v], st_s, st_r, (s, (v + r) % V)).start()
     stat_rx[v] = stat_tx[...]
-    for r in range(1, S):
-        t = (s + r) % S
-        got(ids.at[t], id_r.at[t])
+    got(ids.at[0:S - 1], id_r)
     code_relay(0)
 
     @pl.when(close)
@@ -377,9 +375,7 @@
         embed_ready()
         lax.fori_loop(0, tiles // 2, embed_tile, 0)
 
-    for r in range(1, V):
-        u = (v + r) % V
-        got(stat_rx.at[u], st_r.at[u])
+    got(stat_rx.at[0:V - 1], st_r)
     sums = stat_rx[0]
     for u in range(1, V):
         sums = sums + stat_rx[u]
@@ -648,9 +644,9 @@
         vm((Z, W // 2, T), bf16), vm((W // 2, T), bf16), vm((W // 2, T), bf16), vm((R, Q), f32),
         dma((6,)), *[dma((Z * shares,))] * 4,
         dma, dma((S * shares,)), dma, dma((S * shares,)), dma, dma((S,)),
-        dma((S,)), dma((S,)), dma((S,)), dma, dma((S,)), dma, dma((S,)),
+        dma((S,)), dma((S,)), dma((S,)), dma, dma, dma, dma,
         dma, dma((S,)),
-        dma, dma((3 * steps,)), dma, dma((V,)), dma, dma((5 * steps,)),
+        dma, dma((3 * steps,)), dma, dma, dma, dma((5 * steps,)),
         dma, dma((S,)), dma((S,)), dma((S,)), dma((Z,)), dma((Z,)),
         dma, dma((Z,)), dma, dma,
     ]

time: 76.5 us -> 76.4 us (level)
  no operation moved by 1% of the time
where the time goes in v6:
time: 76.4 us; the launch traced here: 75.3 us
  Pallas kernels  74.7 us (98%)
    pallas_call x1, Pallas kernels, fused(): pl.pallas_call(functools.partial(fused_kernel, (S, V)), out_shape=(jax.Sh...  72.4 us
    pallas_call x1, Pallas kernels, fused(): pl.pallas_call(put_out, out_shape=tuple((jax.ShapeDtypeStruct(x.shape, x....  2.3 us

profile of v6, /device:TPU:6, one launch (start us, length us, event | category | flops | bytes accessed | tf_op | source)
XLA Modules:
  0.0 75.3 jit_solution(15272777988127080575)
XLA Ops:
  0.6 72.4 %fused.1 = (f32[1,128]{1,0:T(1,128)S(1)}, bf16[576,128]{1,0:T(8,128)(2,1)S(1)}, bf16[2048,1152]{1,0:T(8,128)(2,1)S(1)}) custom-call(bf16[576,128]{1,0:T(8,128)(2,1)} %bitcast.7, bf16[576,128]{1,0:T(8,128)(2,1)} %bitcast.8, bf16[2048,1152]{1,0:T(8,128)(2,1)} %slab_hbm.1, s32[1,128]{1,0:T(1,128)} %bitcast.9, s32[1,128]{1,0:T(1,128)} %bitcast.10, f32[1,128]{1,0:T(1,128)} %bitcast.11), custom_call_target="tpu_custom_call" | custom-call | tf_op jit(solution)/shard_map/fused/pallas_call | solution.py:656
  73.0 2.3 %put_out.1 = (f32[1,128]{1,0:T(1,128)}, bf16[576,128]{1,0:T(8,128)(2,1)}, bf16[2048,1152]{1,0:T(8,128)(2,1)}) custom-call(f32[1,128]{1,0:T(1,128)S(1)} %get-tuple-element.9.loss, bf16[576,128]{1,0:T(8,128)(2,1)S(1)} %get-tuple-element.10.hgrad, bf16[2048,1152]{1,0:T(8,128)(2,1)S(1)} %get-tuple-element.11.tied), custom_call_target="tpu_custom_call" | custom-call | tf_op jit(solution)/shard_map/put_out/pallas_call | solution.py:679
